TPU v7x, 32 devices: a whole 2x2x4 slice. The times are simulated.
32 devices in a mesh: replica: 2 (over core), model: 4 (over y, x), copy: 4 (over z).
Axes of the slice: x: 2, y: 2, z: 4, core: 2. Of those that a mesh axis runs over, the one named last changes fastest.
Arguments:
- slope_up: bfloat16 [8, 1280, 5120], P(('copy', 'replica'), None, 'model'), parts along dimension 0, may hold values from -0.875 to 0.875
- slope_down: bfloat16 [8, 5120, 1280], P(('copy', 'replica'), 'model'), parts along dimension 0, may hold values from -0.875 to 0.875
- slope_norm: bfloat16 [8, 1280], P(('copy', 'replica')), parts along dimension 0, may hold values from -8 to 8
- param_up: float32 [5120, 5120], P(('copy', 'replica'), 'model'), parts along dimension 0, may hold values from -0.25 to 0.25
- param_down: float32 [20480, 1280], P(('copy', 'model'), 'replica'), parts along dimension 0, may hold values from -0.125 to 0.125
- param_norm: float32 [5120], P(('copy', 'replica')), parts along dimension 0, may hold values from 0.25 to 1.75
Outputs:
- half_up: bfloat16 [5120, 5120], P('copy', 'model'), parts along dimension 0
- half_down: bfloat16 [20480, 1280], P(('copy', 'model')), parts along dimension 0
- half_norm: bfloat16 [5120], P('copy'), parts along dimension 0
- next_up: float32 [5120, 5120], P(('copy', 'replica'), 'model'), parts along dimension 0
- next_down: float32 [20480, 1280], P(('copy', 'model'), 'replica'), parts along dimension 0
- next_norm: float32 [5120], P(('copy', 'replica')), parts along dimension 0
There are 4 independent parts, one for each index of `copy`. A program takes and returns all parts, laid end to end along the dimension named above; each array names one. Nothing has to cross between parts.
All inputs are finite; a program needn't handle non-finite values.
Results may differ from a plain program's by a relative error of at most 0.011.
Values may be sent and summed in bfloat16 or wider, within the bound.
A program may use at most 128 MiB of HBM per device.

v0:
```python
import functools

import jax
import jax.numpy as jnp
from jax import lax
from jax.experimental import pallas as pl
from jax.experimental.pallas import tpu as pltpu
from jax.sharding import PartitionSpec as P

learn_rate = 0.5


def shards(slope_up, slope_down, slope_norm, param_up, param_down, param_norm):
    mean_up, mean_down = (
        lax.psum_scatter(
            slope_up[0].astype(jnp.float32).astype(jnp.bfloat16),
            "replica",
            scatter_dimension=0,
            tiled=True,
        ).astype(jnp.float32),
        lax.psum_scatter(
            slope_down[0].astype(jnp.float32).astype(jnp.bfloat16),
            "replica",
            scatter_dimension=1,
            tiled=True,
        ).astype(jnp.float32),
    )
    whole_norm = lax.psum(slope_norm[0].astype(jnp.float32), "replica")
    place = lax.axis_index("replica")
    mean_norm = lax.dynamic_slice_in_dim(
        whole_norm, place * param_norm.shape[0], param_norm.shape[0]
    )
    mean_rate = lax.axis_size("replica") ** (-0.5)
    mean_up = mean_up * mean_rate
    mean_down = mean_down * mean_rate
    mean_norm = mean_norm * mean_rate
    own_up, own_down, slope_up_norm, slope_down_norm = lax.psum(
        (
            jnp.sum(param_up * param_up, axis=1, keepdims=True),
            jnp.sum(param_down * param_down, axis=0, keepdims=True),
            jnp.sum(mean_up * mean_up, axis=1, keepdims=True),
            jnp.sum(mean_down * mean_down, axis=0, keepdims=True),
        ),
        "model",
    )
    mean_up = mean_up * (jnp.sqrt(own_up) * lax.rsqrt(slope_up_norm + 1e-06))
    mean_down = mean_down * (jnp.sqrt(own_down) * lax.rsqrt(slope_down_norm + 1e-06))
    next_up = param_up - learn_rate * mean_up
    next_down = param_down - learn_rate * mean_down
    next_norm = param_norm - learn_rate * mean_norm
    half_up, half_down, half_norm = (
        lax.all_gather(next_up.astype(jnp.bfloat16), "replica", axis=0, tiled=True),
        lax.all_gather(next_down.astype(jnp.bfloat16), "replica", axis=1, tiled=True),
        lax.all_gather(next_norm.astype(jnp.bfloat16), "replica", axis=0, tiled=True),
    )
    return (half_up, half_down, half_norm, next_up, next_down, next_norm)


MESH = pl.DeviceIdType.MESH
LANES = 128
ROWS = 32
AHEAD = 6


def update_kernel(
    replicas,
    models,
    slope_up,
    slope_down,
    slope_norm,
    param_up,
    param_down,
    param_norm,
    half_up,
    half_down,
    half_norm,
    next_up,
    next_down,
    next_norm,
    own_up,
    peer_up,
    own_down,
    peer_down,
    own_vec,
    peer_vec,
    own_gain,
    peer_gain,
    sum_vec,
    part,
    got,
    piece,
    got_piece,
    square,
    spread,
    load_sem,
    pair_send,
    pair_recv,
    norm_send,
    norm_recv,
    piece_send,
    piece_recv,
):
    me = lax.axis_index("replica")
    other = 1 - me
    spot = lax.axis_index("model")
    share, inner = param_up.shape
    depth = param_down.shape[0]
    up_chunks = share // LANES
    down_chunks = share // LANES
    down_rows = 4 * ROWS
    mine = pl.multiple_of(me * share, LANES)
    theirs = pl.multiple_of(other * share, LANES)
    rate = replicas ** (-0.5)
    f32 = jnp.float32

    loads = {}

    def load(name, source, target):
        copy = pltpu.make_async_copy(source, target, load_sem.at[len(loads)])
        copy.start()
        loads[name] = copy

    pairs = {}

    def push(name, source, target):
        copy = pltpu.make_async_remote_copy(
            source,
            target,
            pair_send.at[len(pairs)],
            pair_recv.at[len(pairs)],
            device_id={"replica": other},
            device_id_type=MESH,
        )
        copy.start()
        pairs[name] = copy

    def up_rows(c):
        return pl.ds(c * LANES, LANES)

    def down_part(c):
        return pl.ds(c * LANES, LANES)

    load("pu", param_up, next_up)
    load("pd", param_down, next_down)
    for c in range(up_chunks):
        load(
            ("up", c),
            slope_up.at[0, pl.ds(mine + c * LANES, LANES), :],
            own_up.at[up_rows(c), :],
        )
    for c in range(down_chunks):
        load(
            ("down", c),
            slope_down.at[0, :, pl.ds(mine + c * LANES, LANES)],
            own_down.at[:, down_part(c)],
        )
    load("sn", slope_norm, own_vec)
    load("pn", param_norm, own_gain)

    barrier = pltpu.get_barrier_semaphore()
    pl.semaphore_signal(
        barrier, inc=1, device_id={"replica": other}, device_id_type=MESH
    )
    for k in range(1, models):
        pl.semaphore_signal(
            barrier,
            inc=1,
            device_id={"model": lax.rem(spot + k, models)},
            device_id_type=MESH,
        )
    pl.semaphore_wait(barrier, models)

    for c in range(up_chunks):
        push(
            ("up", c),
            slope_up.at[0, pl.ds(theirs + c * LANES, LANES), :],
            peer_up.at[up_rows(c), :],
        )
    for c in range(down_chunks):
        push(
            ("down", c),
            slope_down.at[0, :, pl.ds(theirs + c * LANES, LANES)],
            peer_down.at[:, down_part(c)],
        )
    push("sn", slope_norm, peer_vec)
    push("pn", param_norm, peer_gain)

    sent = []

    def share_norm(source, target, sems, i):
        copies = []
        for k in range(1, models):
            copy = pltpu.make_async_remote_copy(
                source.at[i],
                target.at[i, k - 1],
                sems[0].at[i, k - 1],
                sems[1].at[i, k - 1],
                device_id={"model": lax.rem(spot + k, models)},
                device_id_type=MESH,
            )
            copy.start()
            copies.append(copy)
        sent.extend(copies)

        def whole():
            for copy in copies:
                copy.wait_recv()
            total = source[i]
            for k in range(1, models):
                total = total + target[i, k - 1]
            return total

        return whole

    def share_param(i):
        return share_norm(part, got, (norm_send, norm_recv), i)

    def share_slope(i):
        return share_norm(piece, got_piece, (piece_send, piece_recv), i)

    def row_squares(c, value):
        @pl.loop(0, LANES // ROWS)
        def _(r):
            rows = pl.ds(c * LANES + r * ROWS, ROWS)
            total = jnp.zeros((ROWS, LANES), f32)
            for j in range(inner // LANES):
                x = value(rows, pl.ds(j * LANES, LANES))
                total = total + x * x
            square[pl.ds(r * ROWS, ROWS), :] = total

        return jnp.sum(square[...].T, axis=0, keepdims=True)

    def column_squares(c, value):
        def body(r, total):
            for q in range(down_rows // ROWS):
                x = value(pl.ds(r * down_rows + q * ROWS, ROWS), down_part(c))
                total = total + x * x
            return total

        total = lax.fori_loop(
            0, depth // down_rows, body, jnp.zeros((ROWS, LANES), f32)
        )
        return jnp.sum(total, axis=0, keepdims=True)

    def sum_up(rows, lanes):
        return own_up[rows, lanes].astype(f32) + peer_up[rows, lanes].astype(f32)

    def sum_down(rows, lanes):
        return own_down[rows, lanes].astype(f32) + peer_down[rows, lanes].astype(f32)

    loads["pu"].wait()
    for c in range(up_chunks):
        part[0, :, c * LANES : (c + 1) * LANES] = row_squares(
            c, lambda rows, lanes: next_up[rows, lanes]
        )
    whole_up = share_param(0)

    def measure_down():
        loads["pd"].wait()
        for c in range(down_chunks):
            part[1, :, c * LANES : (c + 1) * LANES] = column_squares(
                c, lambda rows, lanes: next_down[rows, lanes]
            )
        return share_param(1)

    pieces = [("up", c) for c in range(up_chunks)]
    pieces += [("down", c) for c in range(down_chunks)]
    slope_wholes = {}
    param_wholes = {}

    def measure_piece(n):
        kind, c = pieces[n]
        loads[pieces[n]].wait()
        pairs[pieces[n]].wait_recv()
        if kind == "up":
            piece[n] = row_squares(c, lambda rows, lanes: sum_up(rows, lanes) * rate)
        else:
            piece[n] = column_squares(
                c, lambda rows, lanes: sum_down(rows, lanes) * rate
            )
        slope_wholes[n] = share_slope(n)

    def update_piece(n):
        kind, c = pieces[n]
        if kind not in param_wholes:
            total = (whole_up if kind == "up" else whole_down)()
            param_wholes[kind] = jnp.sqrt(total) * (rate * learn_rate)
        ratio = param_wholes[kind][:, c * LANES : (c + 1) * LANES] * lax.rsqrt(
            slope_wholes[n]() + 1e-06
        )
        if kind == "up":
            update_up(c, ratio)
        else:
            update_down(c, ratio)

    def update_up(c, ratio):
        spread[...] = jnp.broadcast_to(ratio, (LANES, LANES)).T

        @pl.loop(0, LANES // ROWS)
        def _(r):
            rows = pl.ds(c * LANES + r * ROWS, ROWS)
            scale = spread[pl.ds(r * ROWS, ROWS), :]
            for j in range(inner // LANES):
                lanes = pl.ds(j * LANES, LANES)
                new = next_up[rows, lanes] - sum_up(rows, lanes) * scale
                next_up[rows, lanes] = new
                half_up[pl.ds(mine + c * LANES + r * ROWS, ROWS), lanes] = new.astype(
                    jnp.bfloat16
                )

        block = half_up.at[pl.ds(mine + c * LANES, LANES), :]
        push(("half_up", c), block, block)

    def update_down(c, ratio):
        scale = jnp.broadcast_to(ratio, (ROWS, LANES))
        lanes = down_part(c)
        place = pl.ds(mine + c * LANES, LANES)

        @pl.loop(0, depth // down_rows)
        def _(r):
            for q in range(down_rows // ROWS):
                rows = pl.ds(r * down_rows + q * ROWS, ROWS)
                new = next_down[rows, lanes] - sum_down(rows, lanes) * scale
                next_down[rows, lanes] = new
                half_down[rows, place] = new.astype(jnp.bfloat16)

        block = half_down.at[:, place]
        push(("half_down", c), block, block)

    ahead = min(AHEAD, len(pieces))
    for n in range(len(pieces) + ahead):
        if n == 2:
            whole_down = measure_down()
        if n < len(pieces):
            measure_piece(n)
        if n >= ahead:
            update_piece(n - ahead)

    loads["sn"].wait()
    loads["pn"].wait()
    pairs["sn"].wait_recv()
    pairs["pn"].wait_recv()
    sum_vec[...] = (
        (own_vec[...].astype(f32) + peer_vec[...].astype(f32)) * rate * learn_rate
    )
    new_gain = own_gain[...].reshape(1, share) - sum_vec[:, pl.ds(mine, share)]
    next_norm[...] = new_gain
    half_norm[:, pl.ds(mine, share)] = new_gain
    half_norm[:, pl.ds(theirs, share)] = (
        peer_gain[...].reshape(1, share) - sum_vec[:, pl.ds(theirs, share)]
    )

    for name, copy in pairs.items():
        copy.wait_send()
        if name[0] in ("half_up", "half_down"):
            copy.wait_recv()
    for copy in sent:
        copy.wait_send()


def write_kernel(
    half_up,
    half_down,
    half_norm,
    next_up,
    next_down,
    next_norm,
    half_up_out,
    half_down_out,
    half_norm_out,
    next_up_out,
    next_down_out,
    next_norm_out,
    sem,
):
    moves = (
        (half_up, half_up_out),
        (half_down, half_down_out),
        (next_up, next_up_out),
        (next_down, next_down_out),
    )
    copies = [
        pltpu.make_async_copy(source, target, sem.at[i])
        for i, (source, target) in enumerate(moves)
    ]
    for copy in copies:
        copy.start()
    half_norm_out[...] = half_norm[...].reshape(half_norm_out.shape).astype(
        jnp.bfloat16
    )
    next_norm_out[...] = next_norm[...].reshape(next_norm_out.shape)
    for copy in copies:
        copy.wait()


def fused(replicas, models, slope_up, slope_down, slope_norm, param_up, param_down, param_norm):
    share, inner = param_up.shape
    depth = param_down.shape[0]
    width = slope_up.shape[1]
    down_chunks = share // LANES
    up_chunks = share // LANES
    moves = up_chunks + down_chunks + 2
    bf16, f32 = jnp.bfloat16, jnp.float32
    hbm = pl.BlockSpec(memory_space=pltpu.HBM)
    vmem = pl.BlockSpec(memory_space=pltpu.VMEM)
    outs = pl.pallas_call(
        functools.partial(update_kernel, replicas, models),
        out_shape=(
            OUT((width, inner), bf16),
            OUT((depth, width), bf16),
            OUT((1, width), f32),
            OUT((share, inner), f32),
            OUT((depth, share), f32),
            OUT((1, share), f32),
        ),
        in_specs=[hbm] * 6,
        out_specs=(vmem,) * 6,
        scratch_shapes=[
            pltpu.VMEM((share, inner), bf16),
            pltpu.VMEM((share, inner), bf16),
            pltpu.VMEM((depth, share), bf16),
            pltpu.VMEM((depth, share), bf16),
            pltpu.VMEM((1, width), bf16),
            pltpu.VMEM((1, width), bf16),
            pltpu.VMEM((share,), f32),
            pltpu.VMEM((share,), f32),
            pltpu.VMEM((1, width), f32),
            pltpu.VMEM((2, 1, share), f32),
            pltpu.VMEM((2, models - 1, 1, share), f32),
            pltpu.VMEM((moves - 2, 1, LANES), f32),
            pltpu.VMEM((moves - 2, models - 1, 1, LANES), f32),
            pltpu.VMEM((LANES, LANES), f32),
            pltpu.VMEM((LANES, LANES), f32),
            pltpu.SemaphoreType.DMA((moves + 2,)),
            pltpu.SemaphoreType.DMA((2 * moves,)),
            pltpu.SemaphoreType.DMA((2 * moves,)),
            pltpu.SemaphoreType.DMA((2, models - 1)),
            pltpu.SemaphoreType.DMA((2, models - 1)),
            pltpu.SemaphoreType.DMA((moves - 2, models - 1)),
            pltpu.SemaphoreType.DMA((moves - 2, models - 1)),
        ],
        compiler_params=pltpu.CompilerParams(
            collective_id=0, has_side_effects=True, vmem_limit_bytes=24 * 2**20
        ),
    )(
        *(
            pltpu.with_memory_space_constraint(x, pltpu.HBM)
            for x in (
                slope_up, slope_down, slope_norm, param_up, param_down, param_norm
            )
        )
    )
    return pl.pallas_call(
        write_kernel,
        out_shape=(
            jax.ShapeDtypeStruct((width, inner), bf16),
            jax.ShapeDtypeStruct((depth, width), bf16),
            jax.ShapeDtypeStruct((width,), bf16),
            jax.ShapeDtypeStruct((share, inner), f32),
            jax.ShapeDtypeStruct((depth, share), f32),
            jax.ShapeDtypeStruct((share,), f32),
        ),
        in_specs=[vmem] * 6,
        out_specs=(hbm, hbm, vmem, hbm, hbm, vmem),
        scratch_shapes=[pltpu.SemaphoreType.DMA((4,))],
        compiler_params=pltpu.CompilerParams(vmem_limit_bytes=24 * 2**20),
    )(*(pltpu.with_memory_space_constraint(x, pltpu.VMEM) for x in outs))


def suits(mesh, *arrays):
    slope_up, param_up, param_down = arrays
    return (
        mesh.shape["replica"] == 2
        and mesh.shape["model"] > 1
        and param_up.shape[0] % LANES == 0
        and param_up.shape[1] % LANES == 0
        and param_down.shape[0] % LANES == 0
    )


def step(mesh, slope_up, slope_down, slope_norm, param_up, param_down, param_norm):
    args = (slope_up, slope_down, slope_norm, param_up, param_down, param_norm)
    if suits(mesh, slope_up, param_up, param_down):
        return fused(mesh.shape["replica"], mesh.shape["model"], *args)
    return shards(*args)


OUT = pltpu.VMEM


def solution(mesh):
    return jax.shard_map(
        functools.partial(step, mesh),
        mesh=mesh,
        in_specs=(
            P(("copy", "replica"), None, "model"),
            P(("copy", "replica"), "model", None),
            P(("copy", "replica"), None),
            P(("copy", "replica"), "model"),
            P(("copy", "model"), "replica"),
            P(("copy", "replica")),
        ),
        out_specs=(
            P("copy", "model"),
            P(("copy", "model"), None),
            P("copy"),
            P(("copy", "replica"), "model"),
            P(("copy", "model"), "replica"),
            P(("copy", "replica")),
        ),
        check_vma=False,
    )
```

profile of v0, /device:TPU:0, one launch (start us, length us, event | category | flops | bytes accessed | tf_op | source)
XLA Modules:
  0.0 22.0 jit_solution(14531814747231090303)
XLA Ops:
  0.6 15.9 %shard_map.109 = (bf16[1280,1280]{1,0:T(8,128)(2,1)S(1)}, bf16[1280,1280]{1,0:T(8,128)(2,1)S(1)}, f32[1,1280]{1,0:T(1,128)S(1)}, f32[640,1280]{1,0:T(8,128)S(1)}...) custom-call(bf16[1,1280,1280]{2,1,0:T(8,128)(2,1)} %slope_up.1, bf16[1,1280,1280]{2,1,0:T(8,128)(2,1)} %slope_down.1, ...), custom_call_target="tpu_custom_call" | custom-call | tf_op jit(solution)/shard_map/pallas_call | solution.py:406
  16.5 5.5 %shard_map.110 = (bf16[1280,1280]{1,0:T(8,128)(2,1)}, bf16[1280,1280]{1,0:T(8,128)(2,1)}, bf16[1280]{0:T(1024)(128)(2,1)}, f32[640,1280]{1,0:T(8,128)}, f32[1280,640]{1,0:T(8,128)}, /*index=5*/f32[640]{0:T(1024)}) custom-call(bf16[1280,1280]{1,0:T(8,128)(2,1)S(1)} %get-tuple-element.12.half_up, bf16[1280,1280]{1,0:T(8,128)(2,1)S(1)} %get-tuple-element.13.half_down, ...), custom_call_target="tpu_custom_call" | custom-call | tf_op jit(solution)/shard_map/pallas_call | solution.py:453
where the time goes:
time: 22.1 us; the launch traced here: 22 us
  Pallas kernels  21.3 us (96%)
  between operations  0.64 us (3%)
    pallas_call x1, Pallas kernels, fused(): pl.pallas_call(functools.partial(update_kernel, replicas, models), out_sh...  15.9 us
    pallas_call x1, Pallas kernels, fused(): pl.pallas_call(write_kernel, out_shape=(jax.ShapeDtypeStruct((width, inne...  5.47 us

commit v1 on v0

--- a/solution.py
+++ b/solution.py
@@ -99,6 +99,8 @@
     norm_recv,
     piece_send,
     piece_recv,
+    pair_ready,
+    model_ready,
 ):
     me = lax.axis_index("replica")
     other = 1 - me
@@ -158,17 +160,43 @@
     load("pn", param_norm, own_gain)
 
     barrier = pltpu.get_barrier_semaphore()
-    pl.semaphore_signal(
-        barrier, inc=1, device_id={"replica": other}, device_id_type=MESH
-    )
-    for k in range(1, models):
+    lead = me == replicas - 1
+
+    @pl.when(lead)
+    def _():
         pl.semaphore_signal(
-            barrier,
-            inc=1,
-            device_id={"model": lax.rem(spot + k, models)},
-            device_id_type=MESH,
-        )
-    pl.semaphore_wait(barrier, models)
+            barrier, inc=1, device_id={"replica": other}, device_id_type=MESH
+        )
+
+    @pl.when(jnp.logical_not(lead))
+    def _():
+        pl.semaphore_wait(barrier, 1)
+        pl.semaphore_signal(
+            pair_ready, inc=1, device_id={"replica": other}, device_id_type=MESH
+        )
+
+    @pl.when(lead)
+    def _():
+        pl.semaphore_wait(pair_ready, 1)
+        for k in range(1, models):
+            pl.semaphore_signal(
+                barrier,
+                inc=1,
+                device_id={"model": lax.rem(spot + k, models)},
+                device_id_type=MESH,
+            )
+
+    def meet_models():
+        @pl.when(lead)
+        def _():
+            pl.semaphore_wait(barrier, models - 1)
+            pl.semaphore_signal(
+                model_ready, inc=1, device_id={"replica": other}, device_id_type=MESH
+            )
+
+        @pl.when(jnp.logical_not(lead))
+        def _():
+            pl.semaphore_wait(model_ready, 1)
 
     for c in range(up_chunks):
         push(
@@ -253,6 +281,7 @@
         part[0, :, c * LANES : (c + 1) * LANES] = row_squares(
             c, lambda rows, lanes: next_up[rows, lanes]
         )
+    meet_models()
     whole_up = share_param(0)
 
     def measure_down():
@@ -438,6 +467,8 @@
             pltpu.SemaphoreType.DMA((2, models - 1)),
             pltpu.SemaphoreType.DMA((moves - 2, models - 1)),
             pltpu.SemaphoreType.DMA((moves - 2, models - 1)),
+            pltpu.SemaphoreType.REGULAR,
+            pltpu.SemaphoreType.REGULAR,
         ],
         compiler_params=pltpu.CompilerParams(
             collective_id=0, has_side_effects=True, vmem_limit_bytes=24 * 2**20

time: 22.1 us -> 22.1 us (level)
  no operation moved by 1% of the time
where the time goes in v1:
time: 22.1 us; the launch traced here: 22 us
  Pallas kernels  21.3 us (96%)
  between operations  0.64 us (3%)
    pallas_call x1, Pallas kernels, fused(): pl.pallas_call(functools.partial(update_kernel, replicas, models), out_sh...  15.9 us
    pallas_call x1, Pallas kernels, fused(): pl.pallas_call(write_kernel, out_shape=(jax.ShapeDtypeStruct((width, inne...  5.47 us

profile of v1, /device:TPU:0, one launch (start us, length us, event | category | flops | bytes accessed | tf_op | source)
XLA Modules:
  0.0 22.0 jit_solution(11379696199280439471)
XLA Ops:
  0.6 15.9 %shard_map.109 = (bf16[1280,1280]{1,0:T(8,128)(2,1)S(1)}, bf16[1280,1280]{1,0:T(8,128)(2,1)S(1)}, f32[1,1280]{1,0:T(1,128)S(1)}, f32[640,1280]{1,0:T(8,128)S(1)}...) custom-call(bf16[1,1280,1280]{2,1,0:T(8,128)(2,1)} %slope_up.1, bf16[1,1280,1280]{2,1,0:T(8,128)(2,1)} %slope_down.1, ...), custom_call_target="tpu_custom_call" | custom-call | tf_op jit(solution)/shard_map/pallas_call | solution.py:435
  16.5 5.5 %shard_map.110 = (bf16[1280,1280]{1,0:T(8,128)(2,1)}, bf16[1280,1280]{1,0:T(8,128)(2,1)}, bf16[1280]{0:T(1024)(128)(2,1)}, f32[640,1280]{1,0:T(8,128)}, f32[1280,640]{1,0:T(8,128)}, /*index=5*/f32[640]{0:T(1024)}) custom-call(bf16[1280,1280]{1,0:T(8,128)(2,1)S(1)} %get-tuple-element.12.half_up, bf16[1280,1280]{1,0:T(8,128)(2,1)S(1)} %get-tuple-element.13.half_down, ...), custom_call_target="tpu_custom_call" | custom-call | tf_op jit(solution)/shard_map/pallas_call | solution.py:484

commit v2 on v1

--- a/solution.py
+++ b/solution.py
@@ -59,7 +59,8 @@
 MESH = pl.DeviceIdType.MESH
 LANES = 128
 ROWS = 32
-AHEAD = 6
+AHEAD = 7
+DOWN_AT = 5
 
 
 def update_kernel(
@@ -86,6 +87,7 @@
     own_gain,
     peer_gain,
     sum_vec,
+    gain,
     part,
     got,
     piece,
@@ -142,22 +144,32 @@
     def down_part(c):
         return pl.ds(c * LANES, LANES)
 
-    load("pu", param_up, next_up)
-    load("pd", param_down, next_down)
-    for c in range(up_chunks):
-        load(
-            ("up", c),
-            slope_up.at[0, pl.ds(mine + c * LANES, LANES), :],
-            own_up.at[up_rows(c), :],
-        )
-    for c in range(down_chunks):
-        load(
-            ("down", c),
-            slope_down.at[0, :, pl.ds(mine + c * LANES, LANES)],
-            own_down.at[:, down_part(c)],
-        )
-    load("sn", slope_norm, own_vec)
-    load("pn", param_norm, own_gain)
+    def load_param_up():
+        for c in range(up_chunks):
+            load(("pu", c), param_up.at[up_rows(c), :], next_up.at[up_rows(c), :])
+
+    def load_slope_up():
+        for c in range(up_chunks):
+            load(
+                ("up", c),
+                slope_up.at[0, pl.ds(mine + c * LANES, LANES), :],
+                own_up.at[up_rows(c), :],
+            )
+
+    def load_rest():
+        for c in range(down_chunks):
+            load(
+                ("down", c),
+                slope_down.at[0, :, pl.ds(mine + c * LANES, LANES)],
+                own_down.at[:, down_part(c)],
+            )
+        load("pd", param_down, next_down)
+        load("sn", slope_norm, own_vec)
+        load("pn", param_norm, own_gain)
+
+    load_param_up()
+    load_slope_up()
+    load_rest()
 
     barrier = pltpu.get_barrier_semaphore()
     lead = me == replicas - 1
@@ -276,8 +288,8 @@
     def sum_down(rows, lanes):
         return own_down[rows, lanes].astype(f32) + peer_down[rows, lanes].astype(f32)
 
-    loads["pu"].wait()
     for c in range(up_chunks):
+        loads[("pu", c)].wait()
         part[0, :, c * LANES : (c + 1) * LANES] = row_squares(
             c, lambda rows, lanes: next_up[rows, lanes]
         )
@@ -356,28 +368,32 @@
         block = half_down.at[:, place]
         push(("half_down", c), block, block)
 
+    def update_norm():
+        loads["sn"].wait()
+        loads["pn"].wait()
+        pairs["sn"].wait_recv()
+        pairs["pn"].wait_recv()
+        sum_vec[...] = (
+            (own_vec[...].astype(f32) + peer_vec[...].astype(f32)) * rate * learn_rate
+        )
+        new_gain = own_gain[...].reshape(1, share) - sum_vec[:, pl.ds(mine, share)]
+        gain[:, pl.ds(mine, share)] = new_gain
+        gain[:, pl.ds(theirs, share)] = (
+            peer_gain[...].reshape(1, share) - sum_vec[:, pl.ds(theirs, share)]
+        )
+        next_norm[...] = new_gain.reshape(share)
+        half_norm[...] = gain[...].reshape(half_norm.shape).astype(jnp.bfloat16)
+
     ahead = min(AHEAD, len(pieces))
     for n in range(len(pieces) + ahead):
-        if n == 2:
+        if n == min(DOWN_AT, up_chunks):
             whole_down = measure_down()
         if n < len(pieces):
             measure_piece(n)
         if n >= ahead:
             update_piece(n - ahead)
-
-    loads["sn"].wait()
-    loads["pn"].wait()
-    pairs["sn"].wait_recv()
-    pairs["pn"].wait_recv()
-    sum_vec[...] = (
-        (own_vec[...].astype(f32) + peer_vec[...].astype(f32)) * rate * learn_rate
-    )
-    new_gain = own_gain[...].reshape(1, share) - sum_vec[:, pl.ds(mine, share)]
-    next_norm[...] = new_gain
-    half_norm[:, pl.ds(mine, share)] = new_gain
-    half_norm[:, pl.ds(theirs, share)] = (
-        peer_gain[...].reshape(1, share) - sum_vec[:, pl.ds(theirs, share)]
-    )
+    update_norm()
+
 
     for name, copy in pairs.items():
         copy.wait_send()
@@ -403,21 +419,26 @@
     sem,
 ):
     moves = (
+        (half_norm, half_norm_out),
+        (next_norm, next_norm_out),
         (half_up, half_up_out),
         (half_down, half_down_out),
         (next_up, next_up_out),
         (next_down, next_down_out),
     )
-    copies = [
-        pltpu.make_async_copy(source, target, sem.at[i])
-        for i, (source, target) in enumerate(moves)
-    ]
+    copies = []
+    for source, target in moves:
+        cuts = 2 if len(source.shape) == 2 else 1
+        rows = source.shape[0] // cuts
+        for i in range(cuts):
+            part = pl.ds(i * rows, rows)
+            copies.append(
+                pltpu.make_async_copy(
+                    source.at[part], target.at[part], sem.at[len(copies)]
+                )
+            )
     for copy in copies:
         copy.start()
-    half_norm_out[...] = half_norm[...].reshape(half_norm_out.shape).astype(
-        jnp.bfloat16
-    )
-    next_norm_out[...] = next_norm[...].reshape(next_norm_out.shape)
     for copy in copies:
         copy.wait()
 
@@ -437,10 +458,10 @@
         out_shape=(
             OUT((width, inner), bf16),
             OUT((depth, width), bf16),
-            OUT((1, width), f32),
+            OUT((width,), bf16),
             OUT((share, inner), f32),
             OUT((depth, share), f32),
-            OUT((1, share), f32),
+            OUT((share,), f32),
         ),
         in_specs=[hbm] * 6,
         out_specs=(vmem,) * 6,
@@ -454,13 +475,14 @@
             pltpu.VMEM((share,), f32),
             pltpu.VMEM((share,), f32),
             pltpu.VMEM((1, width), f32),
+            pltpu.VMEM((1, width), f32),
             pltpu.VMEM((2, 1, share), f32),
             pltpu.VMEM((2, models - 1, 1, share), f32),
             pltpu.VMEM((moves - 2, 1, LANES), f32),
             pltpu.VMEM((moves - 2, models - 1, 1, LANES), f32),
             pltpu.VMEM((LANES, LANES), f32),
             pltpu.VMEM((LANES, LANES), f32),
-            pltpu.SemaphoreType.DMA((moves + 2,)),
+            pltpu.SemaphoreType.DMA((moves + up_chunks + 1,)),
             pltpu.SemaphoreType.DMA((2 * moves,)),
             pltpu.SemaphoreType.DMA((2 * moves,)),
             pltpu.SemaphoreType.DMA((2, models - 1)),
@@ -492,8 +514,8 @@
             jax.ShapeDtypeStruct((share,), f32),
         ),
         in_specs=[vmem] * 6,
-        out_specs=(hbm, hbm, vmem, hbm, hbm, vmem),
-        scratch_shapes=[pltpu.SemaphoreType.DMA((4,))],
+        out_specs=(hbm,) * 6,
+        scratch_shapes=[pltpu.SemaphoreType.DMA((10,))],
         compiler_params=pltpu.CompilerParams(vmem_limit_bytes=24 * 2**20),
     )(*(pltpu.with_memory_space_constraint(x, pltpu.VMEM) for x in outs))
 

time: 22.1 us -> 20.6 us (0.932)
  Pallas kernels: 21.3 us -> 19.8 us
    pallas_call x1, Pallas kernels: 15.9 us -> 15 us  [fused(): pl.pallas_call(functools.partial(update_kernel, replicas, models), out_sh...]
    pallas_call x1, Pallas kernels: 5.47 us -> 4.85 us  [fused(): pl.pallas_call(write_kernel, out_shape=(jax.ShapeDtypeStruct((width, inne...]
where the time goes in v2:
time: 20.6 us; the launch traced here: 20.4 us
  Pallas kernels  19.8 us (96%)
  between operations  0.64 us (3%)
    pallas_call x1, Pallas kernels, fused(): pl.pallas_call(functools.partial(update_kernel, replicas, models), out_sh...  15 us
    pallas_call x1, Pallas kernels, fused(): pl.pallas_call(write_kernel, out_shape=(jax.ShapeDtypeStruct((width, inne...  4.85 us

profile of v2, /device:TPU:0, one launch (start us, length us, event | category | flops | bytes accessed | tf_op | source)
XLA Modules:
  0.0 20.4 jit_solution(17160992945452461857)
XLA Ops:
  0.6 15.0 %shard_map.109 = (bf16[1280,1280]{1,0:T(8,128)(2,1)S(1)}, bf16[1280,1280]{1,0:T(8,128)(2,1)S(1)}, bf16[1280]{0:T(1024)(128)(2,1)S(1)}, f32[640,1280]{1,0:T(8,128...) custom-call(bf16[1,1280,1280]{2,1,0:T(8,128)(2,1)} %slope_up.1, bf16[1,1280,1280]{2,1,0:T(8,128)(2,1)} %slope_down.1, ...), custom_call_target="tpu_custom_call" | custom-call | tf_op jit(solution)/shard_map/pallas_call | solution.py:456
  15.6 4.9 %shard_map.110 = (bf16[1280,1280]{1,0:T(8,128)(2,1)}, bf16[1280,1280]{1,0:T(8,128)(2,1)}, bf16[1280]{0:T(1024)(128)(2,1)}, f32[640,1280]{1,0:T(8,128)}, f32[1280,640]{1,0:T(8,128)}, /*index=5*/f32[640]{0:T(1024)}) custom-call(bf16[1280,1280]{1,0:T(8,128)(2,1)S(1)} %get-tuple-element.12.half_up, bf16[1280,1280]{1,0:T(8,128)(2,1)S(1)} %get-tuple-element.13.half_down, ...), custom_call_target="tpu_custom_call" | custom-call | tf_op jit(solution)/shard_map/pallas_call | solution.py:506

commit v3 on v2

--- a/solution.py
+++ b/solution.py
@@ -59,8 +59,7 @@
 MESH = pl.DeviceIdType.MESH
 LANES = 128
 ROWS = 32
-AHEAD = 7
-DOWN_AT = 5
+AHEAD = 9
 
 
 def update_kernel(
@@ -88,18 +87,14 @@
     peer_gain,
     sum_vec,
     gain,
-    part,
-    got,
     piece,
     got_piece,
     square,
     spread,
     load_sem,
-    pair_send,
-    pair_recv,
-    norm_send,
-    norm_recv,
-    piece_send,
+    send_sem,
+    slope_recv,
+    half_recv,
     piece_recv,
     pair_ready,
     model_ready,
@@ -109,13 +104,12 @@
     spot = lax.axis_index("model")
     share, inner = param_up.shape
     depth = param_down.shape[0]
-    up_chunks = share // LANES
-    down_chunks = share // LANES
     down_rows = 4 * ROWS
     mine = pl.multiple_of(me * share, LANES)
     theirs = pl.multiple_of(other * share, LANES)
     rate = replicas ** (-0.5)
     f32 = jnp.float32
+    pieces = pieces_of(share)
 
     loads = {}
 
@@ -124,52 +118,55 @@
         copy.start()
         loads[name] = copy
 
-    pairs = {}
-
-    def push(name, source, target):
-        copy = pltpu.make_async_remote_copy(
+    def pair_copy(source, target, send, recv):
+        return pltpu.make_async_remote_copy(
             source,
             target,
-            pair_send.at[len(pairs)],
-            pair_recv.at[len(pairs)],
+            send_sem.at[send],
+            recv,
             device_id={"replica": other},
             device_id_type=MESH,
         )
-        copy.start()
-        pairs[name] = copy
-
-    def up_rows(c):
-        return pl.ds(c * LANES, LANES)
-
-    def down_part(c):
-        return pl.ds(c * LANES, LANES)
-
-    def load_param_up():
-        for c in range(up_chunks):
-            load(("pu", c), param_up.at[up_rows(c), :], next_up.at[up_rows(c), :])
-
-    def load_slope_up():
-        for c in range(up_chunks):
+
+    def own_slope(kind, start, size):
+        if kind == "up":
+            return slope_up.at[0, pl.ds(mine + start, size), :]
+        return slope_down.at[0, :, pl.ds(mine + start, size)]
+
+    def peer_slope(kind, start, size):
+        if kind == "up":
+            return slope_up.at[0, pl.ds(theirs + start, size), :]
+        return slope_down.at[0, :, pl.ds(theirs + start, size)]
+
+    def half(kind, start, size):
+        if kind == "up":
+            return half_up.at[pl.ds(start, size), :]
+        return half_down.at[:, pl.ds(start, size)]
+
+    def cut(kind, up, down, start, size):
+        if kind == "up":
+            return up.at[pl.ds(start, size), :]
+        return down.at[:, pl.ds(start, size)]
+
+    first = {}
+    parts = [("down", 0, LANES), ("down", LANES, share - LANES), ("up", 0, share)]
+    for span in parts:
+        if span[2]:
             load(
-                ("up", c),
-                slope_up.at[0, pl.ds(mine + c * LANES, LANES), :],
-                own_up.at[up_rows(c), :],
+                ("param", span),
+                cut(span[0], param_up, param_down, *span[1:]),
+                cut(span[0], next_up, next_down, *span[1:]),
             )
-
-    def load_rest():
-        for c in range(down_chunks):
             load(
-                ("down", c),
-                slope_down.at[0, :, pl.ds(mine + c * LANES, LANES)],
-                own_down.at[:, down_part(c)],
+                ("slope", span),
+                own_slope(*span),
+                cut(span[0], own_up, own_down, *span[1:]),
             )
-        load("pd", param_down, next_down)
-        load("sn", slope_norm, own_vec)
-        load("pn", param_norm, own_gain)
-
-    load_param_up()
-    load_slope_up()
-    load_rest()
+            for piece_span in pieces:
+                if piece_span[0] == span[0] and piece_span[1] == span[1]:
+                    first[piece_span] = span
+    load("slope norm", slope_norm, own_vec)
+    load("param norm", param_norm, own_gain)
 
     barrier = pltpu.get_barrier_semaphore()
     lead = me == replicas - 1
@@ -210,58 +207,47 @@
         def _():
             pl.semaphore_wait(model_ready, 1)
 
-    for c in range(up_chunks):
-        push(
-            ("up", c),
-            slope_up.at[0, pl.ds(theirs + c * LANES, LANES), :],
-            peer_up.at[up_rows(c), :],
-        )
-    for c in range(down_chunks):
-        push(
-            ("down", c),
-            slope_down.at[0, :, pl.ds(theirs + c * LANES, LANES)],
-            peer_down.at[:, down_part(c)],
-        )
-    push("sn", slope_norm, peer_vec)
-    push("pn", param_norm, peer_gain)
-
-    sent = []
-
-    def share_norm(source, target, sems, i):
-        copies = []
+    for n, span in enumerate(pieces):
+        pair_copy(
+            peer_slope(*span),
+            cut(span[0], peer_up, peer_down, *span[1:]),
+            0 if span[0] == "up" else 1,
+            slope_recv.at[n],
+        ).start()
+    norms = [
+        pair_copy(slope_norm, peer_vec, 2, slope_recv.at[len(pieces)]),
+        pair_copy(param_norm, peer_gain, 3, slope_recv.at[len(pieces) + 1]),
+    ]
+    for copy in norms:
+        copy.start()
+
+    def norm_copy(source, target, n, k):
+        return pltpu.make_async_remote_copy(
+            source,
+            target,
+            send_sem.at[6],
+            piece_recv.at[n],
+            device_id={"model": lax.rem(spot + k, models)},
+            device_id_type=MESH,
+        )
+
+    def share_norm(n):
         for k in range(1, models):
-            copy = pltpu.make_async_remote_copy(
-                source.at[i],
-                target.at[i, k - 1],
-                sems[0].at[i, k - 1],
-                sems[1].at[i, k - 1],
-                device_id={"model": lax.rem(spot + k, models)},
-                device_id_type=MESH,
-            )
-            copy.start()
-            copies.append(copy)
-        sent.extend(copies)
-
-        def whole():
-            for copy in copies:
-                copy.wait_recv()
-            total = source[i]
-            for k in range(1, models):
-                total = total + target[i, k - 1]
-            return total
-
-        return whole
-
-    def share_param(i):
-        return share_norm(part, got, (norm_send, norm_recv), i)
-
-    def share_slope(i):
-        return share_norm(piece, got_piece, (piece_send, piece_recv), i)
-
-    def row_squares(c, value):
-        @pl.loop(0, LANES // ROWS)
+            norm_copy(piece.at[n], got_piece.at[n, k - 1], n, k).start()
+
+    def whole_norm(n):
+        norm_copy(got_piece.at[n], got_piece.at[n], n, 1).wait_recv()
+        total = piece[n]
+        for k in range(1, models):
+            total = total + got_piece[n, k - 1]
+        return total
+
+    square[...] = jnp.zeros(square.shape, f32)
+
+    def row_squares(start, size, value):
+        @pl.loop(0, size // ROWS)
         def _(r):
-            rows = pl.ds(c * LANES + r * ROWS, ROWS)
+            rows = pl.ds(start + r * ROWS, ROWS)
             total = jnp.zeros((ROWS, LANES), f32)
             for j in range(inner // LANES):
                 x = value(rows, pl.ds(j * LANES, LANES))
@@ -270,10 +256,10 @@
 
         return jnp.sum(square[...].T, axis=0, keepdims=True)
 
-    def column_squares(c, value):
+    def column_squares(start, size, value):
         def body(r, total):
             for q in range(down_rows // ROWS):
-                x = value(pl.ds(r * down_rows + q * ROWS, ROWS), down_part(c))
+                x = value(pl.ds(r * down_rows + q * ROWS, ROWS), pl.ds(start, size))
                 total = total + x * x
             return total
 
@@ -288,74 +274,63 @@
     def sum_down(rows, lanes):
         return own_down[rows, lanes].astype(f32) + peer_down[rows, lanes].astype(f32)
 
-    for c in range(up_chunks):
-        loads[("pu", c)].wait()
-        part[0, :, c * LANES : (c + 1) * LANES] = row_squares(
-            c, lambda rows, lanes: next_up[rows, lanes]
-        )
-    meet_models()
-    whole_up = share_param(0)
-
-    def measure_down():
-        loads["pd"].wait()
-        for c in range(down_chunks):
-            part[1, :, c * LANES : (c + 1) * LANES] = column_squares(
-                c, lambda rows, lanes: next_down[rows, lanes]
-            )
-        return share_param(1)
-
-    pieces = [("up", c) for c in range(up_chunks)]
-    pieces += [("down", c) for c in range(down_chunks)]
-    slope_wholes = {}
-    param_wholes = {}
-
     def measure_piece(n):
-        kind, c = pieces[n]
-        loads[pieces[n]].wait()
-        pairs[pieces[n]].wait_recv()
+        kind, start, size = pieces[n]
+        squares = row_squares if kind == "up" else column_squares
+        param = next_up if kind == "up" else next_down
+        total = sum_up if kind == "up" else sum_down
+        span = first.get(pieces[n])
+        if span:
+            loads["param", span].wait()
+        piece[n, 0:1] = squares(start, size, lambda rows, lanes: param[rows, lanes])
+        if span:
+            loads["slope", span].wait()
+        pair_copy(
+            peer_slope(*pieces[n]),
+            cut(kind, peer_up, peer_down, start, size),
+            0,
+            slope_recv.at[n],
+        ).wait_recv()
+        piece[n, 1:2] = squares(
+            start, size, lambda rows, lanes: total(rows, lanes) * rate
+        )
+        if n == 0:
+            meet_models()
+        share_norm(n)
+
+    def update_piece(n):
+        kind, start, size = pieces[n]
+        whole = whole_norm(n)
+        ratio = jnp.sqrt(whole[0:1]) * (rate * learn_rate) * lax.rsqrt(
+            whole[1:2] + 1e-06
+        )
         if kind == "up":
-            piece[n] = row_squares(c, lambda rows, lanes: sum_up(rows, lanes) * rate)
+            update_up(start, size, ratio)
         else:
-            piece[n] = column_squares(
-                c, lambda rows, lanes: sum_down(rows, lanes) * rate
-            )
-        slope_wholes[n] = share_slope(n)
-
-    def update_piece(n):
-        kind, c = pieces[n]
-        if kind not in param_wholes:
-            total = (whole_up if kind == "up" else whole_down)()
-            param_wholes[kind] = jnp.sqrt(total) * (rate * learn_rate)
-        ratio = param_wholes[kind][:, c * LANES : (c + 1) * LANES] * lax.rsqrt(
-            slope_wholes[n]() + 1e-06
-        )
-        if kind == "up":
-            update_up(c, ratio)
-        else:
-            update_down(c, ratio)
-
-    def update_up(c, ratio):
+            update_down(start, size, ratio)
+        block = half(kind, mine + start, size)
+        which = 0 if kind == "up" else 1
+        pair_copy(block, block, 4 + which, half_recv.at[which]).start()
+
+    def update_up(start, size, ratio):
         spread[...] = jnp.broadcast_to(ratio, (LANES, LANES)).T
 
-        @pl.loop(0, LANES // ROWS)
+        @pl.loop(0, size // ROWS)
         def _(r):
-            rows = pl.ds(c * LANES + r * ROWS, ROWS)
+            rows = pl.ds(start + r * ROWS, ROWS)
             scale = spread[pl.ds(r * ROWS, ROWS), :]
             for j in range(inner // LANES):
                 lanes = pl.ds(j * LANES, LANES)
                 new = next_up[rows, lanes] - sum_up(rows, lanes) * scale
                 next_up[rows, lanes] = new
-                half_up[pl.ds(mine + c * LANES + r * ROWS, ROWS), lanes] = new.astype(
+                half_up[pl.ds(mine + start + r * ROWS, ROWS), lanes] = new.astype(
                     jnp.bfloat16
                 )
 
-        block = half_up.at[pl.ds(mine + c * LANES, LANES), :]
-        push(("half_up", c), block, block)
-
-    def update_down(c, ratio):
+    def update_down(start, size, ratio):
         scale = jnp.broadcast_to(ratio, (ROWS, LANES))
-        lanes = down_part(c)
-        place = pl.ds(mine + c * LANES, LANES)
+        lanes = pl.ds(start, size)
+        place = pl.ds(mine + start, size)
 
         @pl.loop(0, depth // down_rows)
         def _(r):
@@ -365,14 +340,11 @@
                 next_down[rows, lanes] = new
                 half_down[rows, place] = new.astype(jnp.bfloat16)
 
-        block = half_down.at[:, place]
-        push(("half_down", c), block, block)
-
     def update_norm():
-        loads["sn"].wait()
-        loads["pn"].wait()
-        pairs["sn"].wait_recv()
-        pairs["pn"].wait_recv()
+        loads["slope norm"].wait()
+        loads["param norm"].wait()
+        for copy in norms:
+            copy.wait_recv()
         sum_vec[...] = (
             (own_vec[...].astype(f32) + peer_vec[...].astype(f32)) * rate * learn_rate
         )
@@ -386,21 +358,36 @@
 
     ahead = min(AHEAD, len(pieces))
     for n in range(len(pieces) + ahead):
-        if n == min(DOWN_AT, up_chunks):
-            whole_down = measure_down()
         if n < len(pieces):
             measure_piece(n)
         if n >= ahead:
             update_piece(n - ahead)
     update_norm()
 
-
-    for name, copy in pairs.items():
+    for which, kind in enumerate(("up", "down")):
+        pair_copy(
+            peer_slope(kind, 0, share),
+            cut(kind, peer_up, peer_down, 0, share),
+            which,
+            half_recv.at[which],
+        ).wait_send()
+        halves = pair_copy(
+            half(kind, mine, share),
+            half(kind, theirs, share),
+            4 + which,
+            half_recv.at[which],
+        )
+        halves.wait_send()
+        halves.wait_recv()
+    for copy in norms:
         copy.wait_send()
-        if name[0] in ("half_up", "half_down"):
-            copy.wait_recv()
-    for copy in sent:
-        copy.wait_send()
+    norm_copy(got_piece, got_piece, 0, 1).wait_send()
+
+
+def pieces_of(share):
+    pieces = [("down", start, LANES) for start in range(0, share, LANES)]
+    pieces += [("up", start, LANES) for start in range(0, share, LANES)]
+    return pieces
 
 
 def write_kernel(
@@ -447,9 +434,7 @@
     share, inner = param_up.shape
     depth = param_down.shape[0]
     width = slope_up.shape[1]
-    down_chunks = share // LANES
-    up_chunks = share // LANES
-    moves = up_chunks + down_chunks + 2
+    count = len(pieces_of(share))
     bf16, f32 = jnp.bfloat16, jnp.float32
     hbm = pl.BlockSpec(memory_space=pltpu.HBM)
     vmem = pl.BlockSpec(memory_space=pltpu.VMEM)
@@ -476,19 +461,15 @@
             pltpu.VMEM((share,), f32),
             pltpu.VMEM((1, width), f32),
             pltpu.VMEM((1, width), f32),
-            pltpu.VMEM((2, 1, share), f32),
-            pltpu.VMEM((2, models - 1, 1, share), f32),
-            pltpu.VMEM((moves - 2, 1, LANES), f32),
-            pltpu.VMEM((moves - 2, models - 1, 1, LANES), f32),
+            pltpu.VMEM((count, 2, LANES), f32),
+            pltpu.VMEM((count, models - 1, 2, LANES), f32),
             pltpu.VMEM((LANES, LANES), f32),
             pltpu.VMEM((LANES, LANES), f32),
-            pltpu.SemaphoreType.DMA((moves + up_chunks + 1,)),
-            pltpu.SemaphoreType.DMA((2 * moves,)),
-            pltpu.SemaphoreType.DMA((2 * moves,)),
-            pltpu.SemaphoreType.DMA((2, models - 1)),
-            pltpu.SemaphoreType.DMA((2, models - 1)),
-            pltpu.SemaphoreType.DMA((moves - 2, models - 1)),
-            pltpu.SemaphoreType.DMA((moves - 2, models - 1)),
+            pltpu.SemaphoreType.DMA((8,)),
+            pltpu.SemaphoreType.DMA((7,)),
+            pltpu.SemaphoreType.DMA((count + 2,)),
+            pltpu.SemaphoreType.DMA((2,)),
+            pltpu.SemaphoreType.DMA((count,)),
             pltpu.SemaphoreType.REGULAR,
             pltpu.SemaphoreType.REGULAR,
         ],

time: 20.6 us -> 19.5 us (0.947)
  Pallas kernels: 19.8 us -> 18.7 us
    pallas_call x1, Pallas kernels: 15 us -> 13.8 us  [fused(): pl.pallas_call(functools.partial(update_kernel, replicas, models), out_sh...]
where the time goes in v3:
time: 19.5 us; the launch traced here: 19.3 us
  Pallas kernels  18.7 us (96%)
  between operations  0.64 us (3%)
    pallas_call x1, Pallas kernels, fused(): pl.pallas_call(functools.partial(update_kernel, replicas, models), out_sh...  13.8 us
    pallas_call x1, Pallas kernels, fused(): pl.pallas_call(write_kernel, out_shape=(jax.ShapeDtypeStruct((width, inne...  4.85 us

profile of v3, /device:TPU:0, one launch (start us, length us, event | category | flops | bytes accessed | tf_op | source)
XLA Modules:
  0.0 19.3 jit_solution(7266794777030377887)
XLA Ops:
  0.6 13.8 %shard_map.109 = (bf16[1280,1280]{1,0:T(8,128)(2,1)S(1)}, bf16[1280,1280]{1,0:T(8,128)(2,1)S(1)}, bf16[1280]{0:T(1024)(128)(2,1)S(1)}, f32[640,1280]{1,0:T(8,128...) custom-call(bf16[1,1280,1280]{2,1,0:T(8,128)(2,1)} %slope_up.1, bf16[1,1280,1280]{2,1,0:T(8,128)(2,1)} %slope_down.1, ...), custom_call_target="tpu_custom_call" | custom-call | tf_op jit(solution)/shard_map/pallas_call | solution.py:441
  14.5 4.9 %shard_map.110 = (bf16[1280,1280]{1,0:T(8,128)(2,1)}, bf16[1280,1280]{1,0:T(8,128)(2,1)}, bf16[1280]{0:T(1024)(128)(2,1)}, f32[640,1280]{1,0:T(8,128)}, f32[1280,640]{1,0:T(8,128)}, /*index=5*/f32[640]{0:T(1024)}) custom-call(bf16[1280,1280]{1,0:T(8,128)(2,1)S(1)} %get-tuple-element.12.half_up, bf16[1280,1280]{1,0:T(8,128)(2,1)S(1)} %get-tuple-element.13.half_down, ...), custom_call_target="tpu_custom_call" | custom-call | tf_op jit(solution)/shard_map/pallas_call | solution.py:487

commit v4 on v3

--- a/solution.py
+++ b/solution.py
@@ -59,7 +59,9 @@
 MESH = pl.DeviceIdType.MESH
 LANES = 128
 ROWS = 32
-AHEAD = 9
+AHEAD = 8
+UP_CUTS = 2
+DOWN_CUTS = 2
 
 
 def update_kernel(
@@ -104,7 +106,7 @@
     spot = lax.axis_index("model")
     share, inner = param_up.shape
     depth = param_down.shape[0]
-    down_rows = 4 * ROWS
+    down_rows = 10 * ROWS
     mine = pl.multiple_of(me * share, LANES)
     theirs = pl.multiple_of(other * share, LANES)
     rate = replicas ** (-0.5)
@@ -147,6 +149,22 @@
         if kind == "up":
             return up.at[pl.ds(start, size), :]
         return down.at[:, pl.ds(start, size)]
+
+    barrier = pltpu.get_barrier_semaphore()
+    lead = me == replicas - 1
+
+    @pl.when(lead)
+    def _():
+        pl.semaphore_signal(
+            barrier, inc=1, device_id={"replica": other}, device_id_type=MESH
+        )
+
+    @pl.when(jnp.logical_not(lead))
+    def _():
+        pl.semaphore_wait(barrier, 1)
+        pl.semaphore_signal(
+            pair_ready, inc=1, device_id={"replica": other}, device_id_type=MESH
+        )
 
     first = {}
     parts = [("down", 0, LANES), ("down", LANES, share - LANES), ("up", 0, share)]
@@ -168,22 +186,6 @@
     load("slope norm", slope_norm, own_vec)
     load("param norm", param_norm, own_gain)
 
-    barrier = pltpu.get_barrier_semaphore()
-    lead = me == replicas - 1
-
-    @pl.when(lead)
-    def _():
-        pl.semaphore_signal(
-            barrier, inc=1, device_id={"replica": other}, device_id_type=MESH
-        )
-
-    @pl.when(jnp.logical_not(lead))
-    def _():
-        pl.semaphore_wait(barrier, 1)
-        pl.semaphore_signal(
-            pair_ready, inc=1, device_id={"replica": other}, device_id_type=MESH
-        )
-
     @pl.when(lead)
     def _():
         pl.semaphore_wait(pair_ready, 1)
@@ -245,8 +247,7 @@
     square[...] = jnp.zeros(square.shape, f32)
 
     def row_squares(start, size, value):
-        @pl.loop(0, size // ROWS)
-        def _(r):
+        for r in range(size // ROWS):
             rows = pl.ds(start + r * ROWS, ROWS)
             total = jnp.zeros((ROWS, LANES), f32)
             for j in range(inner // LANES):
@@ -291,9 +292,7 @@
             0,
             slope_recv.at[n],
         ).wait_recv()
-        piece[n, 1:2] = squares(
-            start, size, lambda rows, lanes: total(rows, lanes) * rate
-        )
+        piece[n, 1:2] = squares(start, size, total)
         if n == 0:
             meet_models()
         share_norm(n)
@@ -302,43 +301,52 @@
         kind, start, size = pieces[n]
         whole = whole_norm(n)
         ratio = jnp.sqrt(whole[0:1]) * (rate * learn_rate) * lax.rsqrt(
-            whole[1:2] + 1e-06
+            whole[1:2] * (rate * rate) + 1e-06
         )
         if kind == "up":
             update_up(start, size, ratio)
         else:
             update_down(start, size, ratio)
-        block = half(kind, mine + start, size)
-        which = 0 if kind == "up" else 1
-        pair_copy(block, block, 4 + which, half_recv.at[which]).start()
 
     def update_up(start, size, ratio):
         spread[...] = jnp.broadcast_to(ratio, (LANES, LANES)).T
-
-        @pl.loop(0, size // ROWS)
-        def _(r):
-            rows = pl.ds(start + r * ROWS, ROWS)
-            scale = spread[pl.ds(r * ROWS, ROWS), :]
-            for j in range(inner // LANES):
-                lanes = pl.ds(j * LANES, LANES)
-                new = next_up[rows, lanes] - sum_up(rows, lanes) * scale
-                next_up[rows, lanes] = new
-                half_up[pl.ds(mine + start + r * ROWS, ROWS), lanes] = new.astype(
-                    jnp.bfloat16
-                )
+        per = size // UP_CUTS
+
+        @pl.loop(0, size // per)
+        def _(p):
+            for q in range(per // ROWS):
+                r = p * (per // ROWS) + q
+                rows = pl.ds(start + r * ROWS, ROWS)
+                scale = spread[pl.ds(r * ROWS, ROWS), :]
+                for j in range(inner // LANES):
+                    lanes = pl.ds(j * LANES, LANES)
+                    new = next_up[rows, lanes] - sum_up(rows, lanes) * scale
+                    next_up[rows, lanes] = new
+                    half_up[pl.ds(mine + start + r * ROWS, ROWS), lanes] = new.astype(
+                        jnp.bfloat16
+                    )
+            block = half_up.at[pl.ds(mine + start + p * per, per), :]
+            pair_copy(block, block, 4, half_recv.at[0]).start()
 
     def update_down(start, size, ratio):
         scale = jnp.broadcast_to(ratio, (ROWS, LANES))
         lanes = pl.ds(start, size)
         place = pl.ds(mine + start, size)
 
-        @pl.loop(0, depth // down_rows)
-        def _(r):
-            for q in range(down_rows // ROWS):
-                rows = pl.ds(r * down_rows + q * ROWS, ROWS)
-                new = next_down[rows, lanes] - sum_down(rows, lanes) * scale
-                next_down[rows, lanes] = new
-                half_down[rows, place] = new.astype(jnp.bfloat16)
+        per = depth // DOWN_CUTS
+
+        @pl.loop(0, DOWN_CUTS)
+        def _(p):
+            @pl.loop(0, per // down_rows)
+            def _(r):
+                for q in range(down_rows // ROWS):
+                    rows = pl.ds(p * per + r * down_rows + q * ROWS, ROWS)
+                    new = next_down[rows, lanes] - sum_down(rows, lanes) * scale
+                    next_down[rows, lanes] = new
+                    half_down[rows, place] = new.astype(jnp.bfloat16)
+
+            block = half_down.at[pl.ds(p * per, per), place]
+            pair_copy(block, block, 5, half_recv.at[1]).start()
 
     def update_norm():
         loads["slope norm"].wait()
@@ -413,21 +421,14 @@
         (next_up, next_up_out),
         (next_down, next_down_out),
     )
-    copies = []
-    for source, target in moves:
-        cuts = 2 if len(source.shape) == 2 else 1
+    for i, (source, target) in enumerate(moves):
+        cuts = 8 if len(source.shape) == 2 else 1
         rows = source.shape[0] // cuts
-        for i in range(cuts):
-            part = pl.ds(i * rows, rows)
-            copies.append(
-                pltpu.make_async_copy(
-                    source.at[part], target.at[part], sem.at[len(copies)]
-                )
-            )
-    for copy in copies:
-        copy.start()
-    for copy in copies:
-        copy.wait()
+        for c in range(cuts):
+            part = pl.ds(c * rows, rows)
+            pltpu.make_async_copy(source.at[part], target.at[part], sem.at[i]).start()
+    for i, (source, target) in enumerate(moves):
+        pltpu.make_async_copy(source, target, sem.at[i]).wait()
 
 
 def fused(replicas, models, slope_up, slope_down, slope_norm, param_up, param_down, param_norm):
@@ -496,7 +497,7 @@
         ),
         in_specs=[vmem] * 6,
         out_specs=(hbm,) * 6,
-        scratch_shapes=[pltpu.SemaphoreType.DMA((10,))],
+        scratch_shapes=[pltpu.SemaphoreType.DMA((6,))],
         compiler_params=pltpu.CompilerParams(vmem_limit_bytes=24 * 2**20),
     )(*(pltpu.with_memory_space_constraint(x, pltpu.VMEM) for x in outs))
 

time: 19.5 us -> 19.2 us (0.985)
  Pallas kernels: 18.7 us -> 18.4 us
where the time goes in v4:
time: 19.2 us; the launch traced here: 19.1 us
  Pallas kernels  18.4 us (96%)
  between operations  0.64 us (3%)
    pallas_call x1, Pallas kernels, fused(): pl.pallas_call(functools.partial(update_kernel, replicas, models), out_sh...  13.7 us
    pallas_call x1, Pallas kernels, fused(): pl.pallas_call(write_kernel, out_shape=(jax.ShapeDtypeStruct((width, inne...  4.76 us

profile of v4, /device:TPU:0, one launch (start us, length us, event | category | flops | bytes accessed | tf_op | source)
XLA Modules:
  0.0 19.1 jit_solution(4845477279596752796)
XLA Ops:
  0.6 13.7 %shard_map.109 = (bf16[1280,1280]{1,0:T(8,128)(2,1)S(1)}, bf16[1280,1280]{1,0:T(8,128)(2,1)S(1)}, bf16[1280]{0:T(1024)(128)(2,1)S(1)}, f32[640,1280]{1,0:T(8,128...) custom-call(bf16[1,1280,1280]{2,1,0:T(8,128)(2,1)} %slope_up.1, bf16[1,1280,1280]{2,1,0:T(8,128)(2,1)} %slope_down.1, ...), custom_call_target="tpu_custom_call" | custom-call | tf_op jit(solution)/shard_map/pallas_call | solution.py:442
  14.3 4.8 %shard_map.110 = (bf16[1280,1280]{1,0:T(8,128)(2,1)}, bf16[1280,1280]{1,0:T(8,128)(2,1)}, bf16[1280]{0:T(1024)(128)(2,1)}, f32[640,1280]{1,0:T(8,128)}, f32[1280,640]{1,0:T(8,128)}, /*index=5*/f32[640]{0:T(1024)}) custom-call(bf16[1280,1280]{1,0:T(8,128)(2,1)S(1)} %get-tuple-element.12.half_up, bf16[1280,1280]{1,0:T(8,128)(2,1)S(1)} %get-tuple-element.13.half_down, ...), custom_call_target="tpu_custom_call" | custom-call | tf_op jit(solution)/shard_map/pallas_call | solution.py:488

commit v5 on v4

--- a/solution.py
+++ b/solution.py
@@ -89,6 +89,10 @@
     peer_gain,
     sum_vec,
     gain,
+    lent_param,
+    lent_slope,
+    lent_own,
+    lent_norm,
     piece,
     got_piece,
     square,
@@ -98,6 +102,7 @@
     slope_recv,
     half_recv,
     piece_recv,
+    lent_recv,
     pair_ready,
     model_ready,
 ):
@@ -166,6 +171,7 @@
             pair_ready, inc=1, device_id={"replica": other}, device_id_type=MESH
         )
 
+    spare = share - LANES
     first = {}
     parts = [("down", 0, LANES), ("down", LANES, share - LANES), ("up", 0, share)]
     for span in parts:
@@ -186,6 +192,12 @@
     load("slope norm", slope_norm, own_vec)
     load("param norm", param_norm, own_gain)
 
+    @pl.when(jnp.logical_and(spot == 0, lead))
+    def _():
+        pltpu.make_async_copy(
+            peer_slope("up", spare, LANES), lent_own, load_sem.at[8]
+        ).start()
+
     @pl.when(lead)
     def _():
         pl.semaphore_wait(pair_ready, 1)
@@ -223,6 +235,18 @@
     for copy in norms:
         copy.start()
 
+    last = len(pieces) - 1
+    gives = jnp.logical_and(spot == 0, jnp.logical_not(lead))
+    takes = jnp.logical_and(spot == 0, lead)
+    lent = (
+        pair_copy(param_up.at[pl.ds(spare, LANES), :], lent_param, 8, lent_recv.at[0]),
+        pair_copy(own_slope("up", spare, LANES), lent_slope, 9, lent_recv.at[1]),
+    )
+    @pl.when(gives)
+    def _():
+        for copy in lent:
+            copy.start()
+
     def norm_copy(source, target, n, k):
         return pltpu.make_async_remote_copy(
             source,
@@ -237,12 +261,27 @@
         for k in range(1, models):
             norm_copy(piece.at[n], got_piece.at[n, k - 1], n, k).start()
 
+    def lend_norm(source, target):
+        return pltpu.make_async_remote_copy(
+            source,
+            target,
+            send_sem.at[7],
+            lent_recv.at[2],
+            device_id={"model": 0, "replica": other},
+            device_id_type=MESH,
+        )
+
     def whole_norm(n):
         norm_copy(got_piece.at[n], got_piece.at[n], n, 1).wait_recv()
         total = piece[n]
         for k in range(1, models):
             total = total + got_piece[n, k - 1]
         return total
+
+    def ratio_of(whole):
+        return jnp.sqrt(whole[0:1]) * (rate * learn_rate) * lax.rsqrt(
+            whole[1:2] * (rate * rate) + 1e-06
+        )
 
     square[...] = jnp.zeros(square.shape, f32)
 
@@ -296,13 +335,15 @@
         if n == 0:
             meet_models()
         share_norm(n)
+        if n == last:
+
+            @pl.when(jnp.logical_not(lead))
+            def _():
+                lend_norm(piece.at[n], lent_norm.at[models - 1 - spot]).start()
 
     def update_piece(n):
         kind, start, size = pieces[n]
-        whole = whole_norm(n)
-        ratio = jnp.sqrt(whole[0:1]) * (rate * learn_rate) * lax.rsqrt(
-            whole[1:2] * (rate * rate) + 1e-06
-        )
+        ratio = ratio_of(whole_norm(n))
         if kind == "up":
             update_up(start, size, ratio)
         else:
@@ -325,8 +366,14 @@
                     half_up[pl.ds(mine + start + r * ROWS, ROWS), lanes] = new.astype(
                         jnp.bfloat16
                     )
-            block = half_up.at[pl.ds(mine + start + p * per, per), :]
-            pair_copy(block, block, 4, half_recv.at[0]).start()
+            def push_half():
+                block = half_up.at[pl.ds(mine + start + p * per, per), :]
+                pair_copy(block, block, 4, half_recv.at[0]).start()
+
+            if start == spare:
+                pl.when(jnp.logical_not(gives))(push_half)
+            else:
+                push_half()
 
     def update_down(start, size, ratio):
         scale = jnp.broadcast_to(ratio, (ROWS, LANES))
@@ -372,6 +419,32 @@
             update_piece(n - ahead)
     update_norm()
 
+    @pl.when(takes)
+    def _():
+        for copy in lent:
+            copy.wait_recv()
+        pltpu.make_async_copy(
+            peer_slope("up", spare, LANES), lent_own, load_sem.at[8]
+        ).wait()
+        lend_norm(lent_norm, lent_norm).wait_recv()
+        whole = lent_norm[models - 1]
+        for k in range(1, models):
+            whole = whole + lent_norm[k - 1]
+        spread[...] = jnp.broadcast_to(ratio_of(whole), (LANES, LANES)).T
+
+        @pl.loop(0, LANES // ROWS)
+        def _(r):
+            rows = pl.ds(r * ROWS, ROWS)
+            scale = spread[rows, :]
+            for j in range(inner // LANES):
+                lanes = pl.ds(j * LANES, LANES)
+                total = lent_slope[rows, lanes].astype(f32) + lent_own[
+                    rows, lanes
+                ].astype(f32)
+                half_up[pl.ds(theirs + spare + r * ROWS, ROWS), lanes] = (
+                    lent_param[rows, lanes] - total * scale
+                ).astype(jnp.bfloat16)
+
     for which, kind in enumerate(("up", "down")):
         pair_copy(
             peer_slope(kind, 0, share),
@@ -379,14 +452,43 @@
             which,
             half_recv.at[which],
         ).wait_send()
-        halves = pair_copy(
-            half(kind, mine, share),
-            half(kind, theirs, share),
-            4 + which,
-            half_recv.at[which],
-        )
-        halves.wait_send()
-        halves.wait_recv()
+
+        def halves(size):
+            return pair_copy(
+                half(kind, mine, size),
+                half(kind, theirs, size),
+                4 + which,
+                half_recv.at[which],
+            )
+
+        if kind == "up":
+
+            @pl.when(gives)
+            def _():
+                halves(spare).wait_send()
+                for copy in lent:
+                    copy.wait_send()
+
+            @pl.when(jnp.logical_not(gives))
+            def _():
+                halves(share).wait_send()
+
+            @pl.when(takes)
+            def _():
+                halves(spare).wait_recv()
+
+            @pl.when(jnp.logical_not(takes))
+            def _():
+                halves(share).wait_recv()
+
+        else:
+            halves(share).wait_send()
+            halves(share).wait_recv()
+
+    @pl.when(jnp.logical_not(lead))
+    def _():
+        lend_norm(piece.at[last], lent_norm.at[0]).wait_send()
+
     for copy in norms:
         copy.wait_send()
     norm_copy(got_piece, got_piece, 0, 1).wait_send()
@@ -462,15 +564,20 @@
             pltpu.VMEM((share,), f32),
             pltpu.VMEM((1, width), f32),
             pltpu.VMEM((1, width), f32),
+            pltpu.VMEM((LANES, inner), f32),
+            pltpu.VMEM((LANES, inner), bf16),
+            pltpu.VMEM((LANES, inner), bf16),
+            pltpu.VMEM((models, 2, LANES), f32),
             pltpu.VMEM((count, 2, LANES), f32),
             pltpu.VMEM((count, models - 1, 2, LANES), f32),
             pltpu.VMEM((LANES, LANES), f32),
             pltpu.VMEM((LANES, LANES), f32),
-            pltpu.SemaphoreType.DMA((8,)),
-            pltpu.SemaphoreType.DMA((7,)),
+            pltpu.SemaphoreType.DMA((9,)),
+            pltpu.SemaphoreType.DMA((10,)),
             pltpu.SemaphoreType.DMA((count + 2,)),
             pltpu.SemaphoreType.DMA((2,)),
             pltpu.SemaphoreType.DMA((count,)),
+            pltpu.SemaphoreType.DMA((3,)),
             pltpu.SemaphoreType.REGULAR,
             pltpu.SemaphoreType.REGULAR,
         ],
@@ -508,6 +615,7 @@
         mesh.shape["replica"] == 2
         and mesh.shape["model"] > 1
         and param_up.shape[0] % LANES == 0
+        and param_up.shape[0] > LANES
         and param_up.shape[1] % LANES == 0
         and param_down.shape[0] % LANES == 0
     )

time: 19.2 us -> 18.8 us (0.979)
  Pallas kernels: 18.4 us -> 18 us
    pallas_call x1, Pallas kernels: 13.7 us -> 13.2 us  [fused(): pl.pallas_call(functools.partial(update_kernel, replicas, models), out_sh...]
where the time goes in v5:
time: 18.8 us; the launch traced here: 18.6 us
  Pallas kernels  18 us (96%)
  between operations  0.64 us (3%)
    pallas_call x1, Pallas kernels, fused(): pl.pallas_call(functools.partial(update_kernel, replicas, models), out_sh...  13.2 us
    pallas_call x1, Pallas kernels, fused(): pl.pallas_call(write_kernel, out_shape=(jax.ShapeDtypeStruct((width, inne...  4.76 us

profile of v5, /device:TPU:0, one launch (start us, length us, event | category | flops | bytes accessed | tf_op | source)
XLA Modules:
  0.0 18.6 jit_solution(1121871949212883374)
XLA Ops:
  0.6 13.2 %shard_map.109 = (bf16[1280,1280]{1,0:T(8,128)(2,1)S(1)}, bf16[1280,1280]{1,0:T(8,128)(2,1)S(1)}, bf16[1280]{0:T(1024)(128)(2,1)S(1)}, f32[640,1280]{1,0:T(8,128...) custom-call(bf16[1,1280,1280]{2,1,0:T(8,128)(2,1)} %slope_up.1, bf16[1,1280,1280]{2,1,0:T(8,128)(2,1)} %slope_down.1, ...), custom_call_target="tpu_custom_call" | custom-call | tf_op jit(solution)/shard_map/pallas_call | solution.py:544
  13.9 4.8 %shard_map.110 = (bf16[1280,1280]{1,0:T(8,128)(2,1)}, bf16[1280,1280]{1,0:T(8,128)(2,1)}, bf16[1280]{0:T(1024)(128)(2,1)}, f32[640,1280]{1,0:T(8,128)}, f32[1280,640]{1,0:T(8,128)}, /*index=5*/f32[640]{0:T(1024)}) custom-call(bf16[1280,1280]{1,0:T(8,128)(2,1)S(1)} %get-tuple-element.12.half_up, bf16[1280,1280]{1,0:T(8,128)(2,1)S(1)} %get-tuple-element.13.half_down, ...), custom_call_target="tpu_custom_call" | custom-call | tf_op jit(solution)/shard_map/pallas_call | solution.py:595

commit v6 on v5

--- a/solution.py
+++ b/solution.py
@@ -61,7 +61,7 @@
 ROWS = 32
 AHEAD = 8
 UP_CUTS = 2
-DOWN_CUTS = 2
+DOWN_CUTS = 4
 
 
 def update_kernel(
@@ -111,7 +111,7 @@
     spot = lax.axis_index("model")
     share, inner = param_up.shape
     depth = param_down.shape[0]
-    down_rows = 10 * ROWS
+    down_per, down_rows = steps_of(depth)
     mine = pl.multiple_of(me * share, LANES)
     theirs = pl.multiple_of(other * share, LANES)
     rate = replicas ** (-0.5)
@@ -225,12 +225,12 @@
         pair_copy(
             peer_slope(*span),
             cut(span[0], peer_up, peer_down, *span[1:]),
-            0 if span[0] == "up" else 1,
+            0,
             slope_recv.at[n],
         ).start()
     norms = [
-        pair_copy(slope_norm, peer_vec, 2, slope_recv.at[len(pieces)]),
-        pair_copy(param_norm, peer_gain, 3, slope_recv.at[len(pieces) + 1]),
+        pair_copy(slope_norm, peer_vec, 1, slope_recv.at[len(pieces)]),
+        pair_copy(param_norm, peer_gain, 2, slope_recv.at[len(pieces) + 1]),
     ]
     for copy in norms:
         copy.start()
@@ -239,9 +239,12 @@
     gives = jnp.logical_and(spot == 0, jnp.logical_not(lead))
     takes = jnp.logical_and(spot == 0, lead)
     lent = (
-        pair_copy(param_up.at[pl.ds(spare, LANES), :], lent_param, 8, lent_recv.at[0]),
-        pair_copy(own_slope("up", spare, LANES), lent_slope, 9, lent_recv.at[1]),
-    )
+        pair_copy(param_up.at[pl.ds(spare, LANES), :], lent_param, 6, lent_recv.at[0]),
+        pair_copy(own_slope("up", spare, LANES), lent_slope, 6, lent_recv.at[0]),
+    )
+    both = next_up.at[pl.ds(0, LANES + LANES // 2), :]
+    lent_both = pair_copy(both, both, 6, lent_recv.at[0])
+
     @pl.when(gives)
     def _():
         for copy in lent:
@@ -251,7 +254,7 @@
         return pltpu.make_async_remote_copy(
             source,
             target,
-            send_sem.at[6],
+            send_sem.at[4],
             piece_recv.at[n],
             device_id={"model": lax.rem(spot + k, models)},
             device_id_type=MESH,
@@ -265,8 +268,8 @@
         return pltpu.make_async_remote_copy(
             source,
             target,
-            send_sem.at[7],
-            lent_recv.at[2],
+            send_sem.at[5],
+            lent_recv.at[1],
             device_id={"model": 0, "replica": other},
             device_id_type=MESH,
         )
@@ -368,7 +371,7 @@
                     )
             def push_half():
                 block = half_up.at[pl.ds(mine + start + p * per, per), :]
-                pair_copy(block, block, 4, half_recv.at[0]).start()
+                pair_copy(block, block, 3, half_recv.at[0]).start()
 
             if start == spare:
                 pl.when(jnp.logical_not(gives))(push_half)
@@ -380,9 +383,9 @@
         lanes = pl.ds(start, size)
         place = pl.ds(mine + start, size)
 
-        per = depth // DOWN_CUTS
-
-        @pl.loop(0, DOWN_CUTS)
+        per = down_per
+
+        @pl.loop(0, depth // per)
         def _(p):
             @pl.loop(0, per // down_rows)
             def _(r):
@@ -393,7 +396,7 @@
                     half_down[rows, place] = new.astype(jnp.bfloat16)
 
             block = half_down.at[pl.ds(p * per, per), place]
-            pair_copy(block, block, 5, half_recv.at[1]).start()
+            pair_copy(block, block, 3, half_recv.at[0]).start()
 
     def update_norm():
         loads["slope norm"].wait()
@@ -421,8 +424,7 @@
 
     @pl.when(takes)
     def _():
-        for copy in lent:
-            copy.wait_recv()
+        lent_both.wait_recv()
         pltpu.make_async_copy(
             peer_slope("up", spare, LANES), lent_own, load_sem.at[8]
         ).wait()
@@ -445,45 +447,28 @@
                     lent_param[rows, lanes] - total * scale
                 ).astype(jnp.bfloat16)
 
-    for which, kind in enumerate(("up", "down")):
-        pair_copy(
-            peer_slope(kind, 0, share),
-            cut(kind, peer_up, peer_down, 0, share),
-            which,
-            half_recv.at[which],
-        ).wait_send()
-
-        def halves(size):
-            return pair_copy(
-                half(kind, mine, size),
-                half(kind, theirs, size),
-                4 + which,
-                half_recv.at[which],
-            )
-
-        if kind == "up":
-
-            @pl.when(gives)
-            def _():
-                halves(spare).wait_send()
-                for copy in lent:
-                    copy.wait_send()
-
-            @pl.when(jnp.logical_not(gives))
-            def _():
-                halves(share).wait_send()
-
-            @pl.when(takes)
-            def _():
-                halves(spare).wait_recv()
-
-            @pl.when(jnp.logical_not(takes))
-            def _():
-                halves(share).wait_recv()
-
-        else:
-            halves(share).wait_send()
-            halves(share).wait_recv()
+    pair_copy(half_up, half_up, 0, half_recv.at[0]).wait_send()
+
+    def halves(rows):
+        block = half_up.at[pl.ds(0, rows), :]
+        return pair_copy(block, block, 3, half_recv.at[0])
+
+    @pl.when(gives)
+    def _():
+        halves(2 * share - LANES).wait_send()
+        lent_both.wait_send()
+
+    @pl.when(jnp.logical_not(gives))
+    def _():
+        halves(2 * share).wait_send()
+
+    @pl.when(takes)
+    def _():
+        halves(2 * share - LANES).wait_recv()
+
+    @pl.when(jnp.logical_not(takes))
+    def _():
+        halves(2 * share).wait_recv()
 
     @pl.when(jnp.logical_not(lead))
     def _():
@@ -492,6 +477,12 @@
     for copy in norms:
         copy.wait_send()
     norm_copy(got_piece, got_piece, 0, 1).wait_send()
+
+
+def steps_of(depth):
+    cuts = max(c for c in range(1, DOWN_CUTS + 1) if depth % (c * ROWS) == 0)
+    per = depth // cuts
+    return per, max(k * ROWS for k in range(1, 11) if per % (k * ROWS) == 0)
 
 
 def pieces_of(share):
@@ -573,11 +564,11 @@
             pltpu.VMEM((LANES, LANES), f32),
             pltpu.VMEM((LANES, LANES), f32),
             pltpu.SemaphoreType.DMA((9,)),
-            pltpu.SemaphoreType.DMA((10,)),
+            pltpu.SemaphoreType.DMA((7,)),
             pltpu.SemaphoreType.DMA((count + 2,)),
+            pltpu.SemaphoreType.DMA((1,)),
+            pltpu.SemaphoreType.DMA((count,)),
             pltpu.SemaphoreType.DMA((2,)),
-            pltpu.SemaphoreType.DMA((count,)),
-            pltpu.SemaphoreType.DMA((3,)),
             pltpu.SemaphoreType.REGULAR,
             pltpu.SemaphoreType.REGULAR,
         ],
@@ -616,6 +607,8 @@
         and mesh.shape["model"] > 1
         and param_up.shape[0] % LANES == 0
         and param_up.shape[0] > LANES
+        and param_up.shape[1] == param_down.shape[0]
+        and param_down.shape[1] == param_up.shape[0]
         and param_up.shape[1] % LANES == 0
         and param_down.shape[0] % LANES == 0
     )

time: 18.8 us -> 18.7 us (level)
  no operation moved by 1% of the time
where the time goes in v6:
time: 18.7 us; the launch traced here: 18.5 us
  Pallas kernels  17.9 us (96%)
  between operations  0.64 us (3%)
    pallas_call x1, Pallas kernels, fused(): pl.pallas_call(functools.partial(update_kernel, replicas, models), out_sh...  13.1 us
    pallas_call x1, Pallas kernels, fused(): pl.pallas_call(write_kernel, out_shape=(jax.ShapeDtypeStruct((width, inne...  4.76 us

profile of v6, /device:TPU:0, one launch (start us, length us, event | category | flops | bytes accessed | tf_op | source)
XLA Modules:
  0.0 18.5 jit_solution(15288275049234359026)
XLA Ops:
  0.6 13.1 %shard_map.109 = (bf16[1280,1280]{1,0:T(8,128)(2,1)S(1)}, bf16[1280,1280]{1,0:T(8,128)(2,1)S(1)}, bf16[1280]{0:T(1024)(128)(2,1)S(1)}, f32[640,1280]{1,0:T(8,128...) custom-call(bf16[1,1280,1280]{2,1,0:T(8,128)(2,1)} %slope_up.1, bf16[1,1280,1280]{2,1,0:T(8,128)(2,1)} %slope_down.1, ...), custom_call_target="tpu_custom_call" | custom-call | tf_op jit(solution)/shard_map/pallas_call | solution.py:535
  13.8 4.8 %shard_map.110 = (bf16[1280,1280]{1,0:T(8,128)(2,1)}, bf16[1280,1280]{1,0:T(8,128)(2,1)}, bf16[1280]{0:T(1024)(128)(2,1)}, f32[640,1280]{1,0:T(8,128)}, f32[1280,640]{1,0:T(8,128)}, /*index=5*/f32[640]{0:T(1024)}) custom-call(bf16[1280,1280]{1,0:T(8,128)(2,1)S(1)} %get-tuple-element.12.half_up, bf16[1280,1280]{1,0:T(8,128)(2,1)S(1)} %get-tuple-element.13.half_down, ...), custom_call_target="tpu_custom_call" | custom-call | tf_op jit(solution)/shard_map/pallas_call | solution.py:586

commit v7 on v6

--- a/solution.py
+++ b/solution.py
@@ -59,8 +59,7 @@
 MESH = pl.DeviceIdType.MESH
 LANES = 128
 ROWS = 32
-AHEAD = 8
-UP_CUTS = 2
+AHEAD = 9
 DOWN_CUTS = 4
 
 
@@ -145,11 +144,6 @@
             return slope_up.at[0, pl.ds(theirs + start, size), :]
         return slope_down.at[0, :, pl.ds(theirs + start, size)]
 
-    def half(kind, start, size):
-        if kind == "up":
-            return half_up.at[pl.ds(start, size), :]
-        return half_down.at[:, pl.ds(start, size)]
-
     def cut(kind, up, down, start, size):
         if kind == "up":
             return up.at[pl.ds(start, size), :]
@@ -261,7 +255,8 @@
         )
 
     def share_norm(n):
-        for k in range(1, models):
+        for j in range(models - 1):
+            k = lax.rem(jnp.where(j < spot, j, j + 1) - spot + models, models)
             norm_copy(piece.at[n], got_piece.at[n, k - 1], n, k).start()
 
     def lend_norm(source, target):
@@ -354,29 +349,27 @@
 
     def update_up(start, size, ratio):
         spread[...] = jnp.broadcast_to(ratio, (LANES, LANES)).T
-        per = size // UP_CUTS
-
-        @pl.loop(0, size // per)
-        def _(p):
-            for q in range(per // ROWS):
-                r = p * (per // ROWS) + q
-                rows = pl.ds(start + r * ROWS, ROWS)
-                scale = spread[pl.ds(r * ROWS, ROWS), :]
-                for j in range(inner // LANES):
-                    lanes = pl.ds(j * LANES, LANES)
-                    new = next_up[rows, lanes] - sum_up(rows, lanes) * scale
-                    next_up[rows, lanes] = new
-                    half_up[pl.ds(mine + start + r * ROWS, ROWS), lanes] = new.astype(
-                        jnp.bfloat16
-                    )
-            def push_half():
-                block = half_up.at[pl.ds(mine + start + p * per, per), :]
-                pair_copy(block, block, 3, half_recv.at[0]).start()
-
-            if start == spare:
-                pl.when(jnp.logical_not(gives))(push_half)
-            else:
-                push_half()
+
+        @pl.loop(0, size // ROWS)
+        def _(r):
+            rows = pl.ds(start + r * ROWS, ROWS)
+            scale = spread[pl.ds(r * ROWS, ROWS), :]
+            for j in range(inner // LANES):
+                lanes = pl.ds(j * LANES, LANES)
+                new = next_up[rows, lanes] - sum_up(rows, lanes) * scale
+                next_up[rows, lanes] = new
+                half_up[pl.ds(mine + start + r * ROWS, ROWS), lanes] = new.astype(
+                    jnp.bfloat16
+                )
+
+        def push_half():
+            block = half_up.at[pl.ds(mine + start, size), :]
+            pair_copy(block, block, 3, half_recv.at[0]).start()
+
+        if start == spare:
+            pl.when(jnp.logical_not(gives))(push_half)
+        else:
+            push_half()
 
     def update_down(start, size, ratio):
         scale = jnp.broadcast_to(ratio, (ROWS, LANES))
@@ -418,10 +411,10 @@
     for n in range(len(pieces) + ahead):
         if n < len(pieces):
             measure_piece(n)
+        if n == ahead + 2:
+            update_norm()
         if n >= ahead:
             update_piece(n - ahead)
-    update_norm()
-
     @pl.when(takes)
     def _():
         lent_both.wait_recv()

time: 18.7 us -> 18.8 us (level)
  no operation moved by 1% of the time
where the time goes in v7:
time: 18.8 us; the launch traced here: 18.6 us
  Pallas kernels  18 us (96%)
  between operations  0.64 us (3%)
    pallas_call x1, Pallas kernels, fused(): pl.pallas_call(functools.partial(update_kernel, replicas, models), out_sh...  13.2 us
    pallas_call x1, Pallas kernels, fused(): pl.pallas_call(write_kernel, out_shape=(jax.ShapeDtypeStruct((width, inne...  4.76 us

profile of v7, /device:TPU:0, one launch (start us, length us, event | category | flops | bytes accessed | tf_op | source)
XLA Modules:
  0.0 18.6 jit_solution(9896664269215694736)
XLA Ops:
  0.6 13.2 %shard_map.109 = (bf16[1280,1280]{1,0:T(8,128)(2,1)S(1)}, bf16[1280,1280]{1,0:T(8,128)(2,1)S(1)}, bf16[1280]{0:T(1024)(128)(2,1)S(1)}, f32[640,1280]{1,0:T(8,128...) custom-call(bf16[1,1280,1280]{2,1,0:T(8,128)(2,1)} %slope_up.1, bf16[1,1280,1280]{2,1,0:T(8,128)(2,1)} %slope_down.1, ...), custom_call_target="tpu_custom_call" | custom-call | tf_op jit(solution)/shard_map/pallas_call | solution.py:528
  13.9 4.8 %shard_map.110 = (bf16[1280,1280]{1,0:T(8,128)(2,1)}, bf16[1280,1280]{1,0:T(8,128)(2,1)}, bf16[1280]{0:T(1024)(128)(2,1)}, f32[640,1280]{1,0:T(8,128)}, f32[1280,640]{1,0:T(8,128)}, /*index=5*/f32[640]{0:T(1024)}) custom-call(bf16[1280,1280]{1,0:T(8,128)(2,1)S(1)} %get-tuple-element.12.half_up, bf16[1280,1280]{1,0:T(8,128)(2,1)S(1)} %get-tuple-element.13.half_down, ...), custom_call_target="tpu_custom_call" | custom-call | tf_op jit(solution)/shard_map/pallas_call | solution.py:579

commit v8 on v7

--- a/solution.py
+++ b/solution.py
@@ -59,7 +59,6 @@
 MESH = pl.DeviceIdType.MESH
 LANES = 128
 ROWS = 32
-AHEAD = 9
 DOWN_CUTS = 4
 
 
@@ -96,9 +95,8 @@
     got_piece,
     square,
     spread,
-    load_sem,
+    lent_load,
     send_sem,
-    slope_recv,
     half_recv,
     piece_recv,
     lent_recv,
@@ -117,18 +115,11 @@
     f32 = jnp.float32
     pieces = pieces_of(share)
 
-    loads = {}
-
-    def load(name, source, target):
-        copy = pltpu.make_async_copy(source, target, load_sem.at[len(loads)])
-        copy.start()
-        loads[name] = copy
-
     def pair_copy(source, target, send, recv):
         return pltpu.make_async_remote_copy(
             source,
             target,
-            send_sem.at[send],
+            send,
             recv,
             device_id={"replica": other},
             device_id_type=MESH,
@@ -149,106 +140,23 @@
             return up.at[pl.ds(start, size), :]
         return down.at[:, pl.ds(start, size)]
 
-    barrier = pltpu.get_barrier_semaphore()
     lead = me == replicas - 1
-
-    @pl.when(lead)
-    def _():
-        pl.semaphore_signal(
-            barrier, inc=1, device_id={"replica": other}, device_id_type=MESH
-        )
-
-    @pl.when(jnp.logical_not(lead))
-    def _():
-        pl.semaphore_wait(barrier, 1)
-        pl.semaphore_signal(
-            pair_ready, inc=1, device_id={"replica": other}, device_id_type=MESH
-        )
-
     spare = share - LANES
-    first = {}
-    parts = [("down", 0, LANES), ("down", LANES, share - LANES), ("up", 0, share)]
-    for span in parts:
-        if span[2]:
-            load(
-                ("param", span),
-                cut(span[0], param_up, param_down, *span[1:]),
-                cut(span[0], next_up, next_down, *span[1:]),
-            )
-            load(
-                ("slope", span),
-                own_slope(*span),
-                cut(span[0], own_up, own_down, *span[1:]),
-            )
-            for piece_span in pieces:
-                if piece_span[0] == span[0] and piece_span[1] == span[1]:
-                    first[piece_span] = span
-    load("slope norm", slope_norm, own_vec)
-    load("param norm", param_norm, own_gain)
-
-    @pl.when(jnp.logical_and(spot == 0, lead))
-    def _():
-        pltpu.make_async_copy(
-            peer_slope("up", spare, LANES), lent_own, load_sem.at[8]
-        ).start()
-
-    @pl.when(lead)
-    def _():
-        pl.semaphore_wait(pair_ready, 1)
-        for k in range(1, models):
-            pl.semaphore_signal(
-                barrier,
-                inc=1,
-                device_id={"model": lax.rem(spot + k, models)},
-                device_id_type=MESH,
-            )
-
-    def meet_models():
-        @pl.when(lead)
-        def _():
-            pl.semaphore_wait(barrier, models - 1)
-            pl.semaphore_signal(
-                model_ready, inc=1, device_id={"replica": other}, device_id_type=MESH
-            )
-
-        @pl.when(jnp.logical_not(lead))
-        def _():
-            pl.semaphore_wait(model_ready, 1)
-
-    for n, span in enumerate(pieces):
-        pair_copy(
-            peer_slope(*span),
-            cut(span[0], peer_up, peer_down, *span[1:]),
-            0,
-            slope_recv.at[n],
-        ).start()
-    norms = [
-        pair_copy(slope_norm, peer_vec, 1, slope_recv.at[len(pieces)]),
-        pair_copy(param_norm, peer_gain, 2, slope_recv.at[len(pieces) + 1]),
-    ]
-    for copy in norms:
-        copy.start()
-
     last = len(pieces) - 1
     gives = jnp.logical_and(spot == 0, jnp.logical_not(lead))
     takes = jnp.logical_and(spot == 0, lead)
     lent = (
-        pair_copy(param_up.at[pl.ds(spare, LANES), :], lent_param, 6, lent_recv.at[0]),
-        pair_copy(own_slope("up", spare, LANES), lent_slope, 6, lent_recv.at[0]),
+        pair_copy(param_up.at[pl.ds(spare, LANES), :], lent_param, send_sem.at[3], lent_recv.at[0]),
+        pair_copy(own_slope("up", spare, LANES), lent_slope, send_sem.at[3], lent_recv.at[0]),
     )
     both = next_up.at[pl.ds(0, LANES + LANES // 2), :]
-    lent_both = pair_copy(both, both, 6, lent_recv.at[0])
-
-    @pl.when(gives)
-    def _():
-        for copy in lent:
-            copy.start()
+    lent_both = pair_copy(both, both, send_sem.at[3], lent_recv.at[0])
 
     def norm_copy(source, target, n, k):
         return pltpu.make_async_remote_copy(
             source,
             target,
-            send_sem.at[4],
+            send_sem.at[1],
             piece_recv.at[n],
             device_id={"model": lax.rem(spot + k, models)},
             device_id_type=MESH,
@@ -263,7 +171,7 @@
         return pltpu.make_async_remote_copy(
             source,
             target,
-            send_sem.at[5],
+            send_sem.at[2],
             lent_recv.at[1],
             device_id={"model": 0, "replica": other},
             device_id_type=MESH,
@@ -311,33 +219,6 @@
 
     def sum_down(rows, lanes):
         return own_down[rows, lanes].astype(f32) + peer_down[rows, lanes].astype(f32)
-
-    def measure_piece(n):
-        kind, start, size = pieces[n]
-        squares = row_squares if kind == "up" else column_squares
-        param = next_up if kind == "up" else next_down
-        total = sum_up if kind == "up" else sum_down
-        span = first.get(pieces[n])
-        if span:
-            loads["param", span].wait()
-        piece[n, 0:1] = squares(start, size, lambda rows, lanes: param[rows, lanes])
-        if span:
-            loads["slope", span].wait()
-        pair_copy(
-            peer_slope(*pieces[n]),
-            cut(kind, peer_up, peer_down, start, size),
-            0,
-            slope_recv.at[n],
-        ).wait_recv()
-        piece[n, 1:2] = squares(start, size, total)
-        if n == 0:
-            meet_models()
-        share_norm(n)
-        if n == last:
-
-            @pl.when(jnp.logical_not(lead))
-            def _():
-                lend_norm(piece.at[n], lent_norm.at[models - 1 - spot]).start()
 
     def update_piece(n):
         kind, start, size = pieces[n]
@@ -364,7 +245,7 @@
 
         def push_half():
             block = half_up.at[pl.ds(mine + start, size), :]
-            pair_copy(block, block, 3, half_recv.at[0]).start()
+            pair_copy(block, block, send_sem.at[0], half_recv.at[0]).start()
 
         if start == spare:
             pl.when(jnp.logical_not(gives))(push_half)
@@ -389,37 +270,163 @@
                     half_down[rows, place] = new.astype(jnp.bfloat16)
 
             block = half_down.at[pl.ds(p * per, per), place]
-            pair_copy(block, block, 3, half_recv.at[0]).start()
-
-    def update_norm():
-        loads["slope norm"].wait()
-        loads["param norm"].wait()
+            pair_copy(block, block, send_sem.at[0], half_recv.at[0]).start()
+
+    def exchange(load_sem, early_send, slope_recv):
+        loads = {}
+
+        def load(name, source, target):
+            copy = pltpu.make_async_copy(source, target, load_sem.at[len(loads)])
+            copy.start()
+            loads[name] = copy
+
+        barrier = pltpu.get_barrier_semaphore()
+
+        @pl.when(lead)
+        def _():
+            pl.semaphore_signal(
+                barrier, inc=1, device_id={"replica": other}, device_id_type=MESH
+            )
+
+        @pl.when(jnp.logical_not(lead))
+        def _():
+            pl.semaphore_wait(barrier, 1)
+            pl.semaphore_signal(
+                pair_ready, inc=1, device_id={"replica": other}, device_id_type=MESH
+            )
+
+        first = {}
+        parts = [("down", 0, LANES), ("down", LANES, share - LANES), ("up", 0, share)]
+        for span in parts:
+            if span[2]:
+                load(
+                    ("param", span),
+                    cut(span[0], param_up, param_down, *span[1:]),
+                    cut(span[0], next_up, next_down, *span[1:]),
+                )
+                load(
+                    ("slope", span),
+                    own_slope(*span),
+                    cut(span[0], own_up, own_down, *span[1:]),
+                )
+                for piece_span in pieces:
+                    if piece_span[0] == span[0] and piece_span[1] == span[1]:
+                        first[piece_span] = span
+        load("slope norm", slope_norm, own_vec)
+        load("param norm", param_norm, own_gain)
+
+        @pl.when(jnp.logical_and(spot == 0, lead))
+        def _():
+            pltpu.make_async_copy(
+                peer_slope("up", spare, LANES), lent_own, lent_load.at[0]
+            ).start()
+
+        @pl.when(lead)
+        def _():
+            pl.semaphore_wait(pair_ready, 1)
+            for k in range(1, models):
+                pl.semaphore_signal(
+                    barrier,
+                    inc=1,
+                    device_id={"model": lax.rem(spot + k, models)},
+                    device_id_type=MESH,
+                )
+
+        def meet_models():
+            @pl.when(lead)
+            def _():
+                pl.semaphore_wait(barrier, models - 1)
+                pl.semaphore_signal(
+                    model_ready, inc=1, device_id={"replica": other}, device_id_type=MESH
+                )
+
+            @pl.when(jnp.logical_not(lead))
+            def _():
+                pl.semaphore_wait(model_ready, 1)
+
+        for n, span in enumerate(pieces):
+            pair_copy(
+                peer_slope(*span),
+                cut(span[0], peer_up, peer_down, *span[1:]),
+                early_send.at[0],
+                slope_recv.at[n],
+            ).start()
+        norms = [
+            pair_copy(slope_norm, peer_vec, early_send.at[1], slope_recv.at[len(pieces)]),
+            pair_copy(param_norm, peer_gain, early_send.at[2], slope_recv.at[len(pieces) + 1]),
+        ]
         for copy in norms:
-            copy.wait_recv()
-        sum_vec[...] = (
-            (own_vec[...].astype(f32) + peer_vec[...].astype(f32)) * rate * learn_rate
-        )
-        new_gain = own_gain[...].reshape(1, share) - sum_vec[:, pl.ds(mine, share)]
-        gain[:, pl.ds(mine, share)] = new_gain
-        gain[:, pl.ds(theirs, share)] = (
-            peer_gain[...].reshape(1, share) - sum_vec[:, pl.ds(theirs, share)]
-        )
-        next_norm[...] = new_gain.reshape(share)
-        half_norm[...] = gain[...].reshape(half_norm.shape).astype(jnp.bfloat16)
-
-    ahead = min(AHEAD, len(pieces))
-    for n in range(len(pieces) + ahead):
-        if n < len(pieces):
+            copy.start()
+
+        @pl.when(gives)
+        def _():
+            for copy in lent:
+                copy.start()
+
+        def measure_piece(n):
+            kind, start, size = pieces[n]
+            squares = row_squares if kind == "up" else column_squares
+            param = next_up if kind == "up" else next_down
+            total = sum_up if kind == "up" else sum_down
+            span = first.get(pieces[n])
+            if span:
+                loads["param", span].wait()
+            piece[n, 0:1] = squares(start, size, lambda rows, lanes: param[rows, lanes])
+            if span:
+                loads["slope", span].wait()
+            pair_copy(
+                peer_slope(*pieces[n]),
+                cut(kind, peer_up, peer_down, start, size),
+                early_send.at[0],
+                slope_recv.at[n],
+            ).wait_recv()
+            piece[n, 1:2] = squares(start, size, total)
+            if n == 0:
+                meet_models()
+            share_norm(n)
+            if n == last:
+
+                @pl.when(jnp.logical_not(lead))
+                def _():
+                    lend_norm(piece.at[n], lent_norm.at[models - 1 - spot]).start()
+
+        def update_norm():
+            loads["slope norm"].wait()
+            loads["param norm"].wait()
+            for copy in norms:
+                copy.wait_recv()
+            sum_vec[...] = (
+                (own_vec[...].astype(f32) + peer_vec[...].astype(f32)) * rate * learn_rate
+            )
+            new_gain = own_gain[...].reshape(1, share) - sum_vec[:, pl.ds(mine, share)]
+            gain[:, pl.ds(mine, share)] = new_gain
+            gain[:, pl.ds(theirs, share)] = (
+                peer_gain[...].reshape(1, share) - sum_vec[:, pl.ds(theirs, share)]
+            )
+            next_norm[...] = new_gain.reshape(share)
+            half_norm[...] = gain[...].reshape(half_norm.shape).astype(jnp.bfloat16)
+
+        for n in range(len(pieces)):
             measure_piece(n)
-        if n == ahead + 2:
-            update_norm()
-        if n >= ahead:
-            update_piece(n - ahead)
+        update_norm()
+        pair_copy(half_up, half_up, early_send.at[0], slope_recv.at[0]).wait_send()
+        for copy in norms:
+            copy.wait_send()
+
+    pl.run_scoped(
+        exchange,
+        load_sem=pltpu.SemaphoreType.DMA((8,)),
+        early_send=pltpu.SemaphoreType.DMA((3,)),
+        slope_recv=pltpu.SemaphoreType.DMA((len(pieces) + 2,)),
+    )
+    for n in range(len(pieces)):
+        update_piece(n)
+
     @pl.when(takes)
     def _():
         lent_both.wait_recv()
         pltpu.make_async_copy(
-            peer_slope("up", spare, LANES), lent_own, load_sem.at[8]
+            peer_slope("up", spare, LANES), lent_own, lent_load.at[0]
         ).wait()
         lend_norm(lent_norm, lent_norm).wait_recv()
         whole = lent_norm[models - 1]
@@ -440,11 +447,9 @@
                     lent_param[rows, lanes] - total * scale
                 ).astype(jnp.bfloat16)
 
-    pair_copy(half_up, half_up, 0, half_recv.at[0]).wait_send()
-
     def halves(rows):
         block = half_up.at[pl.ds(0, rows), :]
-        return pair_copy(block, block, 3, half_recv.at[0])
+        return pair_copy(block, block, send_sem.at[0], half_recv.at[0])
 
     @pl.when(gives)
     def _():
@@ -467,8 +472,6 @@
     def _():
         lend_norm(piece.at[last], lent_norm.at[0]).wait_send()
 
-    for copy in norms:
-        copy.wait_send()
     norm_copy(got_piece, got_piece, 0, 1).wait_send()
 
 
@@ -556,9 +559,8 @@
             pltpu.VMEM((count, models - 1, 2, LANES), f32),
             pltpu.VMEM((LANES, LANES), f32),
             pltpu.VMEM((LANES, LANES), f32),
-            pltpu.SemaphoreType.DMA((9,)),
-            pltpu.SemaphoreType.DMA((7,)),
-            pltpu.SemaphoreType.DMA((count + 2,)),
+            pltpu.SemaphoreType.DMA((1,)),
+            pltpu.SemaphoreType.DMA((4,)),
             pltpu.SemaphoreType.DMA((1,)),
             pltpu.SemaphoreType.DMA((count,)),
             pltpu.SemaphoreType.DMA((2,)),

time: 18.8 us -> 18.6 us (0.989)
  Pallas kernels: 18 us -> 17.8 us
    pallas_call x1, Pallas kernels: 13.2 us -> 13 us  [fused(): pl.pallas_call(functools.partial(update_kernel, replicas, models), out_sh...]
where the time goes in v8:
time: 18.6 us; the launch traced here: 18.4 us
  Pallas kernels  17.8 us (96%)
  between operations  0.64 us (3%)
    pallas_call x1, Pallas kernels, fused(): pl.pallas_call(functools.partial(update_kernel, replicas, models), out_sh...  13 us
    pallas_call x1, Pallas kernels, fused(): pl.pallas_call(write_kernel, out_shape=(jax.ShapeDtypeStruct((width, inne...  4.76 us

profile of v8, /device:TPU:0, one launch (start us, length us, event | category | flops | bytes accessed | tf_op | source)
XLA Modules:
  0.0 18.4 jit_solution(1991796729083622720)
XLA Ops:
  0.6 13.0 %shard_map.109 = (bf16[1280,1280]{1,0:T(8,128)(2,1)S(1)}, bf16[1280,1280]{1,0:T(8,128)(2,1)S(1)}, bf16[1280]{0:T(1024)(128)(2,1)S(1)}, f32[640,1280]{1,0:T(8,128...) custom-call(bf16[1,1280,1280]{2,1,0:T(8,128)(2,1)} %slope_up.1, bf16[1,1280,1280]{2,1,0:T(8,128)(2,1)} %slope_down.1, ...), custom_call_target="tpu_custom_call" | custom-call | tf_op jit(solution)/shard_map/pallas_call | solution.py:531
  13.6 4.8 %shard_map.110 = (bf16[1280,1280]{1,0:T(8,128)(2,1)}, bf16[1280,1280]{1,0:T(8,128)(2,1)}, bf16[1280]{0:T(1024)(128)(2,1)}, f32[640,1280]{1,0:T(8,128)}, f32[1280,640]{1,0:T(8,128)}, /*index=5*/f32[640]{0:T(1024)}) custom-call(bf16[1280,1280]{1,0:T(8,128)(2,1)S(1)} %get-tuple-element.12.half_up, bf16[1280,1280]{1,0:T(8,128)(2,1)S(1)} %get-tuple-element.13.half_down, ...), custom_call_target="tpu_custom_call" | custom-call | tf_op jit(solution)/shard_map/pallas_call | solution.py:581

commit v9 on v8

--- a/solution.py
+++ b/solution.py
@@ -152,12 +152,20 @@
     both = next_up.at[pl.ds(0, LANES + LANES // 2), :]
     lent_both = pair_copy(both, both, send_sem.at[3], lent_recv.at[0])
 
+    front = len(pieces) - 3
+    scoped = []
+
+    def norm_recv(n):
+        if scoped and n < front:
+            return scoped[0].at[n]
+        return piece_recv.at[max(n - front, 0)]
+
     def norm_copy(source, target, n, k):
         return pltpu.make_async_remote_copy(
             source,
             target,
             send_sem.at[1],
-            piece_recv.at[n],
+            norm_recv(n),
             device_id={"model": lax.rem(spot + k, models)},
             device_id_type=MESH,
         )
@@ -413,13 +421,20 @@
         for copy in norms:
             copy.wait_send()
 
-    pl.run_scoped(
-        exchange,
-        load_sem=pltpu.SemaphoreType.DMA((8,)),
-        early_send=pltpu.SemaphoreType.DMA((3,)),
-        slope_recv=pltpu.SemaphoreType.DMA((len(pieces) + 2,)),
-    )
-    for n in range(len(pieces)):
+    def begin(front_recv):
+        scoped.append(front_recv)
+        pl.run_scoped(
+            exchange,
+            load_sem=pltpu.SemaphoreType.DMA((8,)),
+            early_send=pltpu.SemaphoreType.DMA((3,)),
+            slope_recv=pltpu.SemaphoreType.DMA((len(pieces) + 2,)),
+        )
+        for n in range(front):
+            update_piece(n)
+        scoped.clear()
+
+    pl.run_scoped(begin, front_recv=pltpu.SemaphoreType.DMA((front,)))
+    for n in range(front, len(pieces)):
         update_piece(n)
 
     @pl.when(takes)
@@ -562,7 +577,7 @@
             pltpu.SemaphoreType.DMA((1,)),
             pltpu.SemaphoreType.DMA((4,)),
             pltpu.SemaphoreType.DMA((1,)),
-            pltpu.SemaphoreType.DMA((count,)),
+            pltpu.SemaphoreType.DMA((3,)),
             pltpu.SemaphoreType.DMA((2,)),
             pltpu.SemaphoreType.REGULAR,
             pltpu.SemaphoreType.REGULAR,

time: 18.6 us -> 18.5 us (level)
  no operation moved by 1% of the time
where the time goes in v9:
time: 18.5 us; the launch traced here: 18.3 us
  Pallas kernels  17.7 us (96%)
  between operations  0.64 us (3%)
    pallas_call x1, Pallas kernels, fused(): pl.pallas_call(functools.partial(update_kernel, replicas, models), out_sh...  12.9 us
    pallas_call x1, Pallas kernels, fused(): pl.pallas_call(write_kernel, out_shape=(jax.ShapeDtypeStruct((width, inne...  4.76 us

profile of v9, /device:TPU:0, one launch (start us, length us, event | category | flops | bytes accessed | tf_op | source)
XLA Modules:
  0.0 18.3 jit_solution(12930953005507421744)
XLA Ops:
  0.6 12.9 %shard_map.109 = (bf16[1280,1280]{1,0:T(8,128)(2,1)S(1)}, bf16[1280,1280]{1,0:T(8,128)(2,1)S(1)}, bf16[1280]{0:T(1024)(128)(2,1)S(1)}, f32[640,1280]{1,0:T(8,128...) custom-call(bf16[1,1280,1280]{2,1,0:T(8,128)(2,1)} %slope_up.1, bf16[1,1280,1280]{2,1,0:T(8,128)(2,1)} %slope_down.1, ...), custom_call_target="tpu_custom_call" | custom-call | tf_op jit(solution)/shard_map/pallas_call | solution.py:546
  13.6 4.8 %shard_map.110 = (bf16[1280,1280]{1,0:T(8,128)(2,1)}, bf16[1280,1280]{1,0:T(8,128)(2,1)}, bf16[1280]{0:T(1024)(128)(2,1)}, f32[640,1280]{1,0:T(8,128)}, f32[1280,640]{1,0:T(8,128)}, /*index=5*/f32[640]{0:T(1024)}) custom-call(bf16[1280,1280]{1,0:T(8,128)(2,1)S(1)} %get-tuple-element.12.half_up, bf16[1280,1280]{1,0:T(8,128)(2,1)S(1)} %get-tuple-element.13.half_down, ...), custom_call_target="tpu_custom_call" | custom-call | tf_op jit(solution)/shard_map/pallas_call | solution.py:596
